TPU v7x, 256 devices: a whole 4x4x8 slice. The times are simulated.
256 devices in a mesh: aperture: 4 (over x), tile: 64 (over y, z, core).
Axes of the slice: x: 4, y: 4, z: 8, core: 2. Of those that a mesh axis runs over, the one named last changes fastest.
Arguments:
- sectors: bfloat16 [4, 768, 512, 2, 512], P('aperture', 'tile'), may hold values from -6 to 6
- footprint: int32 [4, 768, 2], P('aperture', 'tile'), may hold values from 0 to 6, as said below
- own_blocks: bfloat16 [6, 512, 512], replicated, may hold values from -0.25 to 0.25
- edge_blocks: bfloat16 [6, 128, 512], replicated, may hold values from -0.25 to 0.25
- edges: int32 [512, 2], P(('aperture', 'tile')), may hold values from 0 to 32768, as said below
Outputs:
- image: float32 [2, 512, 32768], P(None, ('aperture', 'tile'))
Inputs may be any that keep to these rules, and one draw needn't show every extreme that they name: `footprint`: per device, each group's 12 slots at one tile position hold first the live slots (own entry below 6), then dead ones with both entries 6; at least one slot is live; in every draw some device has all 12 slots live. The edge entry is 6 for every slot at the last tile position. `edges`: each interval spans at least 64 cells; in every draw some line starts at 0 and some line ends at 32768.
All inputs are finite; a program needn't handle non-finite values.
Results may differ from a plain program's by a relative error of at most 0.0003.
Values sent between devices are 32-bit elements; how exact they have to be, the bound alone decides.
No kernel may reach another device: no remote copies, remote signals or barrier semaphores. Data moves between devices by JAX's collectives and lax.ppermute only.
A program may use at most 128 MiB of HBM per device.

v0:
```python
import math

import jax
import jax.numpy as jnp
from jax import lax
from jax.sharding import PartitionSpec as P

GORDER = 8


def from_behind(block, axis, distance):
    devices = range(lax.axis_size(axis))
    route = [(i - distance, i) for i in devices if i - distance in devices]
    return lax.ppermute(block, axis, route)


def gegen_fix(field, edges):
    width = field.shape[-1]
    cells = jnp.arange(width, dtype=jnp.int32)[None, :]
    lower = edges[:, 0:1]
    upper = edges[:, 1:2]
    span = (upper - lower).astype(jnp.float32)
    inside = (cells >= lower) & (cells < upper)
    offset = (cells - lower).astype(jnp.float32)
    xi_vals = jnp.where(inside, -1.0 + (2.0 * offset + 1.0) / span, 0.0)
    base = 1.0 - xi_vals * xi_vals
    weight = jnp.where(inside, base * jnp.sqrt(base), 0.0)
    prev = jnp.ones_like(xi_vals)
    curr = 4.0 * xi_vals
    rebuilt = jnp.zeros_like(field)
    for order in range(GORDER):
        poly = prev if order == 0 else curr
        numer = jnp.sum(weight * poly * field, axis=-1)
        denom = jnp.sum(weight * poly * poly, axis=-1)
        rebuilt = rebuilt + (numer / denom)[..., None] * poly
        if order >= 1:
            nxt = (2.0 * (order + 2) * xi_vals * curr - (order + 3) * prev) / (order + 1)
            prev, curr = (curr, nxt)
    return jnp.where(inside, rebuilt, field)


def phase_table(first, second, modulus):
    left = jnp.arange(first, dtype=jnp.int32)[:, None]
    right = jnp.arange(second, dtype=jnp.int32)[None, :]
    angle = 2.0 * math.pi / modulus * (left * right % modulus).astype(jnp.float32)
    return (jnp.cos(angle), jnp.sin(angle))


def spectral(field, tiles):
    lines = field.shape[1]
    width = field.shape[2]
    inner = width // tiles
    blocks = field.reshape(2, lines, tiles, inner)
    real_part, imag_part = (blocks[0], blocks[1])
    best = lax.Precision.HIGHEST
    cos_outer, sin_outer = phase_table(tiles, tiles, tiles)
    g_real = jnp.einsum("pt,ctm->cpm", cos_outer, real_part, precision=best) - jnp.einsum(
        "pt,ctm->cpm", sin_outer, imag_part, precision=best
    )
    g_imag = jnp.einsum("pt,ctm->cpm", sin_outer, real_part, precision=best) + jnp.einsum(
        "pt,ctm->cpm", cos_outer, imag_part, precision=best
    )
    cos_twist, sin_twist = phase_table(tiles, inner, width)
    h_real = g_real * cos_twist - g_imag * sin_twist
    h_imag = g_real * sin_twist + g_imag * cos_twist
    cos_inner, sin_inner = phase_table(inner, inner, inner)
    z_real = jnp.einsum("qm,cpm->cqp", cos_inner, h_real, precision=best) - jnp.einsum(
        "qm,cpm->cqp", sin_inner, h_imag, precision=best
    )
    z_imag = jnp.einsum("qm,cpm->cqp", sin_inner, h_real, precision=best) + jnp.einsum(
        "qm,cpm->cqp", cos_inner, h_imag, precision=best
    )
    scale = 1.0 / math.sqrt(width)
    return jnp.stack([z_real, z_imag]).reshape(2, lines, width) * scale


def on_device(sectors, footprint, own_blocks, edge_blocks, edges):
    data = sectors[0]
    foot = footprint[0]
    slots = data.shape[0]
    count_blocks = own_blocks.shape[0]
    tile_rows = own_blocks.shape[1]
    edge_rows = edge_blocks.shape[1]
    lines = data.shape[3]
    dims = (((0,), (1,)), ((), ()))

    def apply_kernel(block, kernel):
        return lax.dot_general(block, kernel, dims, preferred_element_type=jnp.float32)

    def visit(slot, carry):
        total, rim = carry
        block = lax.dynamic_index_in_dim(data, slot, 0, keepdims=False)
        own_index = foot[slot, 0]
        edge_index = foot[slot, 1]
        own_kernel = own_blocks[jnp.minimum(own_index, count_blocks - 1)]
        edge_kernel = edge_blocks[jnp.minimum(edge_index, count_blocks - 1)]
        total = total + jnp.where(own_index < count_blocks, apply_kernel(block, own_kernel), 0.0)
        rim = rim + jnp.where(edge_index < count_blocks, apply_kernel(block, edge_kernel), 0.0)
        return (total, rim)

    start = (
        jnp.zeros((2, lines, tile_rows), jnp.float32),
        jnp.zeros((2, lines, edge_rows), jnp.float32),
    )
    total, rim = lax.fori_loop(0, slots, visit, start)
    incoming = from_behind(rim, "tile", 1)
    total = jnp.concatenate([total[:, :, :edge_rows] + incoming, total[:, :, edge_rows:]], axis=2)
    groups = lax.axis_size("aperture")
    tiles = lax.axis_size("tile")
    per_device = lines // (groups * tiles)
    stacked = total.reshape(2, groups, tiles, per_device, tile_rows)
    moved = lax.all_to_all(stacked, "tile", split_axis=2, concat_axis=4, tiled=True)
    summed = lax.psum_scatter(moved, "aperture", scatter_dimension=1, tiled=True)
    field = spectral(summed.reshape(2, per_device, -1), tiles)
    return gegen_fix(field, edges)


def solution(mesh):
    in_specs = (
        P("aperture", "tile", None, None, None),
        P("aperture", "tile", None),
        P(),
        P(),
        P(("aperture", "tile"), None),
    )
    out_specs = P(None, ("aperture", "tile"), None)
    return jax.shard_map(
        on_device, mesh=mesh, in_specs=in_specs, out_specs=out_specs, check_vma=False
    )
```

profile of v0, /device:TPU:1, one launch (start us, length us, event | category | flops | bytes accessed | tf_op | source)
XLA Modules:
  0.0 311.1 jit_solution(1503624357167203079)
XLA Ops:
  6.5 30.9 %copy.13 = bf16[1,12,512,2,512]{2,4,3,1,0:T(8,128)(2,1)} copy(bf16[1,12,512,2,512]{4,3,2,1,0:T(2,128)(2,1)} %param.7) | data formatting | bytes 25165824 | tf_op args[0]
  37.5 89.4 %while.16 = (s32[]{:T(128)}, f32[2,512,512]{2,1,0:T(8,128)S(1)}, f32[2,512,128]{2,1,0:T(8,128)S(1)}, s32[12,2]{0,1:T(2,128)S(1)}, bf16[12,512,2,512]{1,3,2,0:T(8...) while((s32[]{:T(128)}, f32[2,512,512]{2,1,0:T(8,128)S(1)}, ...), condition=%wide.region_1.2_spmd.clone, body=%wide.region_0.1_spmd.clone.sunk | while | flops 673054720 | bytes 7997706 | solution.py:105
  39.5 2.4 select_add_fusion.2
  47.0 2.4 select_add_fusion.2
  54.4 2.4 select_add_fusion.2
  61.9 2.4 select_add_fusion.2
  69.3 2.4 select_add_fusion.2
  76.8 2.4 select_add_fusion.2
  84.2 2.4 select_add_fusion.2
  91.7 2.4 select_add_fusion.2
  99.1 2.4 select_add_fusion.2
  106.6 2.4 select_add_fusion.2
  126.9 4.9 %collective-permute-start = (f32[2,512,128]{2,1,0:T(8,128)S(1)}, f32[2,512,128]{2,1,0:T(8,128)S(1)}, u32[]{:S(2)}, u32[]{:S(2)}) collective-permute-start(f32[2,512,128]{2,1,0:T(8,128)S(1)} %get-tuple-element.131), channel_id=1, source_target_pairs={{0,1},{1,2},{2,3},{3,4},{4,5},{5,6},{6,7},{7,8},{8,9},{9,10},{10,1... | collective-permute-start | bytes 1572872 | tf_op jit(solution)/shard_map/ppermute | solution.py:14
  132.0 6.0 %collective-permute-done = f32[2,512,128]{2,1,0:T(8,128)S(1)} collective-permute-done((f32[2,512,128]{2,1,0:T(8,128)S(1)}, f32[2,512,128]{2,1,0:T(8,128)S(1)}, u32[]{:S(2)}, u32[]{:S(2)}) %collective-permute-start) | collective-permute-done | bytes 524320 | tf_op jit(solution)/shard_map/ppermute | solution.py:14
  139.9 2.6 copy.15
  142.6 13.9 %all-to-all-start = ((f32[2,4,64,2,512]{4,3,1,0,2:T(2,128)}), f32[2,4,64,2,512]{4,3,1,0,2:T(2,128)S(1)}, u32[]{:S(2)}, u32[]{:S(2)}) async-start(f32[2,4,64,2,512]{4,3,1,0,2:T(2,128)} %copy.15), calls=%async_computation | async-start | bytes 4194304 | tf_op jit(solution)/shard_map/all_to_all | solution.py:112
  156.8 51.0 %all-to-all-done = f32[2,4,64,2,512]{4,3,1,0,2:T(2,128)S(1)} async-done(((f32[2,4,64,2,512]{4,3,1,0,2:T(2,128)}), f32[2,4,64,2,512]{4,3,1,0,2:T(2,128)S(1)}, u32[]{:S(2)}, u32[]{:S(2)}) %all-to-all-start) | async-done | bytes 2097184 | tf_op jit(solution)/shard_map/all_to_all | solution.py:112
  211.8 7.9 %broadcast_multiply_fusion.4 = (f32[2,32768]{1,0:T(2,128)S(1)}, f32[2,32768]{1,0:T(2,128)S(1)}, f32[2,32768]{1,0:T(2,128)S(1)}, f32[2,32768]{1,0:T(2,128)}, f32[...) fusion(f32[2]{0:T(128)S(1)} %convert_reduce_fusion, ...), kind=kLoop, calls=%fused_computation.97 | loop fusion | flops 4849648 | bytes 3932248 | tf_op jit(solution)/shard_map/mul | solution.py:29
  219.7 50.3 %all-reduce.3.cloned.1.call-done = f32[2,4,1,2,32768]{4,3,2,1,0:T(2,128)} async-done(((f32[2,4,1,2,32768]{4,3,2,1,0:T(2,128)}), f32[2,4,1,2,32768]{4,3,2,1,0:T(2,128)}) %all-reduce.3.cloned.1.call-update) | async-done | bytes 2097168
  273.9 5.0 %fusion.18 = f32[2,64,512]{2,1,0:T(8,128)S(1)} fusion(f32[2,64,512]{2,1,0:T(8,128)S(1)} %fusion.11, f32[2,64,512]{2,1,0:T(8,128)S(1)} %fusion.12, f32[64,512]{1,0:T(8,128)S(1)} %get-tuple-element.215, f32[64,512]{1,0:T(8,128)S(1)} %get-tuple-element.216), kind=kOutput, calls=%fused_computation.30 | convolution fusion | flops 406519808 | bytes 1048576 | tf_op jit(solution)/shard_map/qm,cpm->cqp/dot_general | solution.py:70
  278.9 5.7 %fusion.22 = f32[2,64,512]{2,1,0:T(8,128)} fusion(f32[2,64,512]{2,1,0:T(8,128)S(1)} %fusion.11, f32[2,64,512]{2,1,0:T(8,128)S(1)} %fusion.12, f32[64,512]{1,0:T(8,128)S(1)} %get-tuple-element.215, f32[64,512]{1,0:T(8,128)S(1)} %get-tuple-element.216), kind=kOutput, calls=%fused_computation.34 | convolution fusion | flops 406519808 | bytes 1048576 | tf_op jit(solution)/shard_map/qm,cpm->cqp/dot_general | solution.py:67
  284.6 5.2 %fusion.13 = f32[2,512,64]{1,2,0:T(8,128)S(1)} fusion(f32[2,64,512]{2,1,0:T(8,128)S(1)} %fusion.18, f32[2,64,512]{2,1,0:T(8,128)S(1)} %fusion.11, f32[2,64,512]{2,1,0:T(8,128)S(1)} %fusion.12, f32[64,512]{1,0:T(8,128)S(1)} %get-tuple-element.215, f32[64,512]{1,0:T(8,128)S(1)} %get-tuple-element.216), kind=kOutput, calls=%fused_computation.24 | convolution fusion | flops 406585344 | bytes 1310720 | tf_op jit(solution)/shard_map/qm,cpm->cqp/dot_general | solution.py:70
  290.3 6.9 %fusion.14 = f32[2,512,64]{1,2,0:T(8,128)} fusion(f32[2,64,512]{2,1,0:T(8,128)} %fusion.22, f32[2,64,512]{2,1,0:T(8,128)} %copy-done, f32[2,64,512]{2,1,0:T(8,128)S(1)} %fusion.12, f32[64,512]{1,0:T(8,128)} %copy-done.1, f32[64,512]{1,0:T(8,128)} %copy-done.2), kind=kOutput, calls=%fused_computation.26 | convolution fusion | flops 406585344 | bytes 1310720 | tf_op jit(solution)/shard_map/qm,cpm->cqp/dot_general | solution.py:67
  298.7 3.4 %multiply_reduce_fusion.7 = (f32[2,2]{1,0:T(2,128)S(1)}, f32[2,2]{1,0:T(2,128)S(1)}, f32[2,2]{1,0:T(2,128)S(1)}, f32[2,2]{1,0:T(2,128)S(1)}, f32[2,2]{1,0:T(2,12...) fusion(f32[2,2,32768]{2,1,0:T(2,128)S(1)} %constant_dynamic-update-slice_fusion, ...), kind=kLoop, calls=%fused_computation.47 | loop fusion | flops 2097120 | bytes 2621568 | tf_op jit(solution)/shard_map/reduce_sum | solution.py:33
  (84 shorter events, 48.0 us)
Async XLA Ops:
  6.5 30.9 %copy-start.3 = (s32[1,12,2]{1,2,0:T(2,128)S(1)}, s32[1,12,2]{1,2,0:T(2,128)}, u32[]{:S(2)}) copy-start(s32[1,12,2]{1,2,0:T(2,128)} %param.8) | copy-start | bytes 292
  126.9 11.0 %collective-permute-start = (f32[2,512,128]{2,1,0:T(8,128)S(1)}, f32[2,512,128]{2,1,0:T(8,128)S(1)}, u32[]{:S(2)}, u32[]{:S(2)}) collective-permute-start(f32[2,512,128]{2,1,0:T(8,128)S(1)} %get-tuple-element.131), channel_id=1, source_target_pairs={{0,1},{1,2},{2,3},{3,4},{4,5},{5,6},{6,7},{7,8},{8,9},{9,10},{10,1... | collective-permute-start | bytes 1572872 | tf_op jit(solution)/shard_map/ppermute | solution.py:14
  142.6 14.0 %copy-start.4 = (s32[2,2]{1,0:T(2,128)S(1)}, s32[2,2]{1,0:T(2,128)}, u32[]{:S(2)}) copy-start(s32[2,2]{1,0:T(2,128)} %param.11) | copy-start | bytes 52
  142.6 65.2 %all-to-all-start = ((f32[2,4,64,2,512]{4,3,1,0,2:T(2,128)}), f32[2,4,64,2,512]{4,3,1,0,2:T(2,128)S(1)}, u32[]{:S(2)}, u32[]{:S(2)}) async-start(f32[2,4,64,2,512]{4,3,1,0,2:T(2,128)} %copy.15), calls=%async_computation | async-start | bytes 4194304 | tf_op jit(solution)/shard_map/all_to_all | solution.py:112
  156.5 113.5 %all-reduce.3.cloned.1.call-start = ((), (), s32[]{:S(2)}) async-start(), calls=%async_computation.1 | async-start | bytes 4194304
  209.8 0.7 copy-start.11
  211.8 72.9 %copy-start.1 = (f32[64,512]{1,0:T(8,128)}, f32[64,512]{1,0:T(8,128)S(1)}, u32[]{:S(2)}) copy-start(f32[64,512]{1,0:T(8,128)S(1)} %get-tuple-element.215) | copy-start | bytes 393220
  211.8 72.8 %copy-start.2 = (f32[64,512]{1,0:T(8,128)}, f32[64,512]{1,0:T(8,128)S(1)}, u32[]{:S(2)}) copy-start(f32[64,512]{1,0:T(8,128)S(1)} %get-tuple-element.216) | copy-start | bytes 393220
  273.9 10.7 %copy-start = (f32[2,64,512]{2,1,0:T(8,128)}, f32[2,64,512]{2,1,0:T(8,128)S(1)}, u32[]{:S(2)}) copy-start(f32[2,64,512]{2,1,0:T(8,128)S(1)} %fusion.11) | copy-start | bytes 786436
  298.3 3.9 %copy-start.6 = (f32[2]{0:T(128)S(1)}, f32[2]{0:T(128)}, u32[]{:S(2)}) copy-start(f32[2]{0:T(128)} %get-tuple-element.201) | copy-start | bytes 28
  298.3 3.9 %copy-start.5 = (f32[2]{0:T(128)S(1)}, f32[2]{0:T(128)}, u32[]{:S(2)}) copy-start(f32[2]{0:T(128)} %get-tuple-element.202) | copy-start | bytes 28
  298.6 3.5 %copy-start.10 = (f32[2]{0:T(128)S(1)}, f32[2]{0:T(128)}, u32[]{:S(2)}) copy-start(f32[2]{0:T(128)} %get-tuple-element.205) | copy-start | bytes 28
  298.6 3.5 %copy-start.9 = (f32[2]{0:T(128)S(1)}, f32[2]{0:T(128)}, u32[]{:S(2)}) copy-start(f32[2]{0:T(128)} %get-tuple-element.198) | copy-start | bytes 28
  298.6 3.5 %copy-start.8 = (f32[2]{0:T(128)S(1)}, f32[2]{0:T(128)}, u32[]{:S(2)}) copy-start(f32[2]{0:T(128)} %get-tuple-element.199) | copy-start | bytes 28
  298.7 3.5 %copy-start.7 = (f32[2]{0:T(128)S(1)}, f32[2]{0:T(128)}, u32[]{:S(2)}) copy-start(f32[2]{0:T(128)} %get-tuple-element.200) | copy-start | bytes 28
Sparse Core Ops, SparseCore 0:
  209.9 60.0 all-reduce.2
where the time goes:
time: 313 us; the launch traced here: 311 us
  waiting for transfers between devices  107 us (34%)
  matrix products  75.1 us (24%)
  local copies, waits for them, and re-layouts  50 us (16%)
  loops' own time  31.4 us (10%)
  starting transfers between devices  18.9 us (6%)
  other arithmetic  14.7 us (5%)
  between operations  13.7 us (4%)
    all_to_all x1, waiting for transfers between devices, on_device(): lax.all_to_all(stacked, 'tile', split_axis=2, concat_axis=4, tiled=True)  51 us
    unnamed x2, waiting for transfers between devices  50.3 us
    dot_general x24, matrix products, apply_kernel(): lax.dot_general(block, kernel, dims, preferred_element_type=jnp.float32)  50.2 us
    unnamed x27, local copies, waits for them, and re-layouts  31.9 us
    another operation x1, loops' own time, on_device(): total, rim = lax.fori_loop(0, slots, visit, start)  31.4 us
    all_to_all x1, starting transfers between devices, on_device(): lax.all_to_all(stacked, 'tile', split_axis=2, concat_axis=4, tiled=True)  13.9 us
    mul x1, other arithmetic, gegen_fix(): curr = 4.0 * xi_vals  7.92 us
    dynamic_slice x12, local copies, waits for them, and re-layouts, visit(): edge_index = foot[slot, 1]  7.86 us
  transfers between devices with their start and end apart: 3, of which 3 were waited for; matrix products, arithmetic and copies ran while one was open for 3% of the time, Pallas kernels for 0%

commit v1 on v0

v1 whole, which is shorter than its diff:
```python
import functools
import math

import jax
import jax.numpy as jnp
import numpy as np
from jax import lax
from jax.experimental import pallas as pl
from jax.experimental.pallas import tpu as pltpu
from jax.sharding import PartitionSpec as P

GORDER = 8
LANES = 128
f32, bf16 = jnp.float32, jnp.bfloat16


def vmem():
    return pl.BlockSpec(memory_space=pltpu.VMEM)


def position(part, relative):
    return (relative - 1) & 3 if part == 0 else 3 - relative


def slot_kernel(cfg, foot, x_hbm, own_hbm, edge_hbm, low_ref, high_ref, rim_ref, xs, owns, edges, wide0, wide1, sems, bsem):
    slots, blocks, rows, erows = cfg
    me = lax.axis_index("aperture")
    depth = x_hbm.shape[1] // 8
    count = jnp.int32(0)
    for s in range(slots):
        count = count + (foot[2 * s] < blocks).astype(jnp.int32)

    def fetch(s):
        return pltpu.make_async_copy(x_hbm.at[s], xs.at[s], sems.at[s])

    own_copy = pltpu.make_async_copy(own_hbm, owns, bsem.at[0])
    edge_copy = pltpu.make_async_copy(edge_hbm, edges, bsem.at[1])
    fetch(0).start()
    own_copy.start()
    edge_copy.start()
    for s in range(1, slots):
        @pl.when(s < count)
        def _():
            fetch(s).start()
    low_ref[...] = jnp.zeros_like(low_ref)
    high_ref[...] = jnp.zeros_like(high_ref)
    rim_ref[...] = jnp.zeros_like(rim_ref)

    def widen(s, wide):
        wide[...] = xs[s].astype(f32)

    def multiply(s, wide):
        e = foot[2 * s + 1]
        keep = (e < blocks).astype(bf16)
        kern = jnp.concatenate([owns[foot[2 * s]], edges[jnp.minimum(e, blocks - 1)] * keep], axis=0)
        for p in range(2):
            x = jnp.concatenate(
                [wide[pl.ds(2 * j + p, depth, stride=8), :].astype(bf16) for j in range(4)], axis=1
            )
            y = jnp.dot(kern, x, preferred_element_type=f32)
            for d in range(4):
                pos = position(p, me ^ d)
                part = y[:, d * LANES:(d + 1) * LANES]
                low_ref[p, pos] += part[:erows]
                high_ref[p, pos] += part[erows:rows]
                rim_ref[p, pos] += part[rows:]

    fetch(0).wait()
    widen(0, wide0)
    own_copy.wait()
    edge_copy.wait()

    def step(s, here, there):
        @pl.when(s + 1 < count)
        def _():
            fetch(s + 1).wait()
        widen(jnp.minimum(s + 1, count - 1), there)
        multiply(s, here)

    def pair(t, carry):
        step(2 * t, wide0, wide1)

        @pl.when(2 * t + 1 < count)
        def _():
            step(2 * t + 1, wide1, wide0)
        return carry
    lax.fori_loop(0, (count + 1) // 2, pair, 0)


def slot_terms(sectors, foot, own, edge):
    slots, depth, parts, lines = sectors.shape
    blocks, rows, _ = own.shape
    erows = edge.shape[1]
    quarter = lines // 4
    sectors = sectors.reshape(slots, depth, 2, 4, LANES).transpose(0, 1, 3, 2, 4).reshape(slots, depth * 8, LANES)
    hbm = pl.BlockSpec(memory_space=pltpu.HBM)
    return pl.pallas_call(
        functools.partial(slot_kernel, (slots, blocks, rows, erows)),
        in_specs=[pl.BlockSpec(memory_space=pltpu.SMEM), hbm, hbm, hbm],
        out_specs=[vmem()] * 3,
        out_shape=[jax.ShapeDtypeStruct((2, 4, r, quarter), f32) for r in (erows, rows - erows, erows)],
        scratch_shapes=[
            pltpu.VMEM((slots, depth * 8, LANES), bf16),
            pltpu.VMEM((blocks, rows, depth), bf16),
            pltpu.VMEM((blocks, erows, depth), bf16),
            pltpu.VMEM((depth * 8, LANES), f32),
            pltpu.VMEM((depth * 8, LANES), f32),
            pltpu.SemaphoreType.DMA((slots,)),
            pltpu.SemaphoreType.DMA((2,)),
        ],
        compiler_params=pltpu.CompilerParams(vmem_limit_bytes=40 << 20),
        cost_estimate=pl.CostEstimate(
            flops=4 * slots * depth * lines * (rows + erows), bytes_accessed=slots * depth * lines * 4, transcendentals=0
        ),
        name="slot_terms",
    )(foot, sectors, own, edge)


def pack_kernel(low_ref, high_ref, la, lb, ha, hb, lqa, lqb, hqa, hqb, out_ref):
    erows = low_ref.shape[2]
    for p, (lr, hr, lq, hq) in enumerate(((la, ha, lqa, hqa), (lb, hb, lqb, hqb))):
        low = low_ref[p, 3] + lr[0] + lq[...]
        out_ref[pl.ds(4 * p, LANES, stride=8), :] = low.T
        for j in range(high_ref.shape[2] // LANES):
            at = pl.ds(j * LANES, LANES)
            high = high_ref[p, 3, at] + hr[0, at] + hq[at]
            out_ref[pl.ds(4 * p + 1 + j, LANES, stride=8), :] = high.T


def pack(*args):
    return pl.pallas_call(
        pack_kernel,
        in_specs=[vmem()] * len(args),
        out_specs=vmem(),
        out_shape=jax.ShapeDtypeStruct((8 * LANES, LANES), f32),
        name="pack",
    )(*args)


def split(x):
    high = x.astype(bf16)
    return high, (x - high.astype(f32)).astype(bf16)


def tables(tiles, width):
    inner = width // LANES
    def wave(a, b, n):
        angle = 2.0 * math.pi / n * ((np.asarray(a)[:, None] * np.asarray(b)[None, :]) % n)
        return np.cos(angle), np.sin(angle)
    a = np.concatenate([2 * np.arange(tiles), 2 * np.arange(tiles) + 1])
    c, s = wave(np.arange(LANES), a, LANES)
    first = np.block([[c, -s], [s, c]])
    c, s = wave(np.arange(inner), np.arange(inner), inner)
    second = np.block([[c, -s], [s, c]])
    c, s = wave(np.arange(LANES), np.arange(inner), width)
    scale = 1.0 / math.sqrt(width)
    def halves(x):
        x = x.astype(np.float32)
        high = x.astype(jnp.bfloat16)
        return high, (x - high.astype(np.float32)).astype(jnp.bfloat16)
    return (*halves(first), *halves(second), (c * scale).astype(np.float32), (s * scale).astype(np.float32))


def image_kernel(edges, x_ref, f_hi, f_lo, s_hi, s_lo, tw_c, tw_s, out_ref, z_ref):
    tiles = x_ref.shape[0] // 16
    inner = tw_c.shape[1]

    def product(high, low, x, dims):
        xh, xl = split(x)
        dot = lambda a, b: lax.dot_general(a, b, dims, preferred_element_type=f32)
        return dot(high, xh) + dot(high, xl) + dot(low, xh)

    columns = []
    for line in range(2):
        stack = []
        for p in range(2):
            for h in range(2):
                stack.append(jnp.concatenate(
                    [x_ref[pl.ds(line * 8 + p * 4 + 2 * h + j, tiles, stride=16), :] for j in range(2)], axis=1))
        columns.append(jnp.concatenate(stack, axis=0))
    x = jnp.concatenate(columns, axis=1)
    g = product(f_hi[...], f_lo[...], x, (((1,), (0,)), ((), ())))
    rows = []
    for line in range(2):
        real = g[:LANES, line * inner:(line + 1) * inner]
        imag = g[LANES:, line * inner:(line + 1) * inner]
        c, s = tw_c[...], tw_s[...]
        rows.append(jnp.concatenate([real * c - imag * s, real * s + imag * c], axis=1))
    z_ref[...] = product(s_hi[...], s_lo[...], jnp.concatenate(rows, axis=0), (((1,), (1,)), ((), ())))

    step = 16
    chunk = step * LANES
    cell = (lax.broadcasted_iota(jnp.int32, (step, LANES), 0) * LANES
            + lax.broadcasted_iota(jnp.int32, (step, LANES), 1))

    for line in range(2):
        lower, upper = edges[line, 0], edges[line, 1]
        span = (upper - lower).astype(f32)
        at = pl.ds(line * LANES, LANES)

        def basis(i):
            n = cell + i * chunk
            inside = (n >= lower) & (n < upper)
            xi = jnp.where(inside, -1.0 + (2.0 * (n - lower).astype(f32) + 1.0) / span, 0.0)
            polys = [jnp.ones_like(xi), 4.0 * xi]
            for k in range(1, GORDER - 1):
                polys.append((2.0 * (k + 2) * xi * polys[k] - (k + 3) * polys[k - 1]) / (k + 1))
            return inside, xi, polys

        def gather(i, sums):
            inside, xi, polys = basis(i)
            base = 1.0 - xi * xi
            weight = jnp.where(inside, base * jnp.sqrt(base), 0.0)
            field = [z_ref[pl.ds(c * inner + i * step, step), at] for c in range(2)]
            out = []
            for k in range(GORDER):
                w = weight * polys[k]
                out += [sums[3 * k] + w * field[0], sums[3 * k + 1] + w * field[1], sums[3 * k + 2] + w * polys[k]]
            return tuple(out)

        begin, end = lower // chunk, (upper + chunk - 1) // chunk
        zero = jnp.zeros((step, LANES), f32)
        sums = lax.fori_loop(begin, end, gather, (zero,) * (3 * GORDER))
        total = [jnp.sum(jnp.sum(v, axis=0, keepdims=True), axis=1, keepdims=True) for v in sums]
        coef = [(total[3 * k] / total[3 * k + 2], total[3 * k + 1] / total[3 * k + 2]) for k in range(GORDER)]

        def rebuild(i, carry):
            inside, xi, polys = basis(i)
            for c in range(2):
                rebuilt = coef[0][c] * polys[0]
                for k in range(1, GORDER):
                    rebuilt = rebuilt + coef[k][c] * polys[k]
                rows = pl.ds(c * inner + i * step, step)
                z_ref[rows, at] = jnp.where(inside, rebuilt, z_ref[rows, at])
            return carry
        lax.fori_loop(begin, end, rebuild, 0)
        for c in range(2):
            out_ref[c, pl.ds(line, inner, stride=2), :] = z_ref[c * inner:(c + 1) * inner, at]


def image(edges, x, width):
    tiles = x.shape[0] // 16
    inner = width // LANES
    consts = [jnp.asarray(t) for t in tables(tiles, width)]
    out = pl.pallas_call(
        image_kernel,
        in_specs=[pl.BlockSpec(memory_space=pltpu.SMEM)] + [vmem()] * 7,
        out_specs=vmem(),
        out_shape=jax.ShapeDtypeStruct((2, 2 * inner, LANES), f32),
        scratch_shapes=[pltpu.VMEM((2 * inner, 2 * LANES), f32)],
        compiler_params=pltpu.CompilerParams(vmem_limit_bytes=24 << 20),
        name="image",
    )(edges, x, *consts)
    return out.reshape(2, inner, 2, LANES).transpose(0, 2, 1, 3).reshape(2, 2, width)


def swap(block, flip):
    return lax.ppermute(block, "aperture", [(i, i ^ flip) for i in range(4)])


def on_device(sectors, footprint, own_blocks, edge_blocks, edges):
    tiles = lax.axis_size("tile")
    low, high, rim = slot_terms(sectors[0], footprint.reshape(-1), own_blocks, edge_blocks)
    incoming = lax.ppermute(rim, "tile", [(i, i + 1) for i in range(tiles - 1)])
    ha, hb = swap(high[0, :2], 1), swap(high[1, :2], 3)
    low = low + incoming
    la, lb = swap(low[0, :2], 1), swap(low[1, :2], 3)
    hqa, hqb = swap(high[0, 2] + ha[1], 3), swap(high[1, 2] + hb[1], 1)
    lqa, lqb = swap(low[0, 2] + la[1], 3), swap(low[1, 2] + lb[1], 1)
    packed = pack(low, high, la, lb, ha, hb, lqa, lqb, hqa, hqb)
    moved = lax.all_to_all(packed.reshape(tiles, 16, LANES), "tile", 0, 0, tiled=True)
    return image(edges, moved.reshape(tiles * 16, LANES), tiles * own_blocks.shape[1])


def solution(mesh):
    in_specs = (
        P("aperture", "tile", None, None, None),
        P("aperture", "tile", None),
        P(),
        P(),
        P(("aperture", "tile"), None),
    )
    out_specs = P(None, ("aperture", "tile"), None)
    return jax.shard_map(
        on_device, mesh=mesh, in_specs=in_specs, out_specs=out_specs, check_vma=False
    )
```

time: 313 us -> 85.3 us (0.27)
  waiting for transfers between devices: 107 us -> 12.9 us
  matrix products: 75.1 us -> 0 us
  local copies, waits for them, and re-layouts: 50 us -> 4.01 us
  blocking collectives: 0 us -> 44.3 us
  loops' own time: 31.4 us -> 0 us
  other arithmetic: 14.7 us -> 0.13 us
  between operations: 13.7 us -> 0.19 us
  Pallas kernels: 0 us -> 9.68 us
  starting transfers between devices: 18.9 us -> 13.5 us
    dot_general x32 -> x0, matrix products: 75.1 us -> none  [the longest x24 50.2 us: apply_kernel(): lax.dot_general(block, kernel, dims, preferred_element_type=jnp.float32)]
    all_to_all x1 -> x0, waiting for transfers between devices: 51 us -> none  [on_device(): lax.all_to_all(stacked, 'tile', split_axis=2, concat_axis=4, tiled=True)]
    unnamed x2 -> x0, waiting for transfers between devices: 50.3 us -> none
    all_to_all x0 -> x1, blocking collectives: none -> 44.3 us  [on_device(): lax.all_to_all(packed.reshape(tiles, 16, LANES), 'tile', 0, 0, tiled=True)]
    another operation x1 -> x0, loops' own time: 31.4 us -> none  [on_device(): total, rim = lax.fori_loop(0, slots, visit, start)]
    unnamed x27 -> x35, local copies, waits for them, and re-layouts: 31.9 us -> 3.85 us
    all_to_all x1 -> x0, starting transfers between devices: 13.9 us -> none  [on_device(): lax.all_to_all(stacked, 'tile', split_axis=2, concat_axis=4, tiled=True)]
    pallas_call x0 -> x3, Pallas kernels: none -> 9.68 us  [the longest x1 3.45 us: slot_terms(): pl.pallas_call(functools.partial(slot_kernel, (slots, blocks, rows, erows...]
  transfers between devices with their start and end apart: 3 -> 9, of which waited for: 3 -> 8; matrix products, arithmetic and copies ran while one was open for 3% -> 0% of each run, Pallas kernels for 0% -> 0%
where the time goes in v1:
time: 85.3 us; the launch traced here: 84.8 us
  blocking collectives  44.3 us (52%)
  starting transfers between devices  13.5 us (16%)
  waiting for transfers between devices  12.9 us (15%)
  Pallas kernels  9.68 us (11%)
  local copies, waits for them, and re-layouts  4.01 us (5%)
    all_to_all x1, blocking collectives, on_device(): lax.all_to_all(packed.reshape(tiles, 16, LANES), 'tile', 0, 0, tiled=True)  44.3 us
    ppermute x8, waiting for transfers between devices, swap(): return lax.ppermute(block, 'aperture', [(i, i ^ flip) for i in range(4)])  9.47 us
    ppermute x8, starting transfers between devices, swap(): return lax.ppermute(block, 'aperture', [(i, i ^ flip) for i in range(4)])  8.58 us
    ppermute x1, starting transfers between devices, on_device(): incoming = lax.ppermute(rim, 'tile', [(i, i + 1) for i in range(tiles - 1)])  4.92 us
    unnamed x35, local copies, waits for them, and re-layouts  3.85 us
    ppermute x1, waiting for transfers between devices, on_device(): incoming = lax.ppermute(rim, 'tile', [(i, i + 1) for i in range(tiles - 1)])  3.48 us
    pallas_call x1, Pallas kernels, slot_terms(): pl.pallas_call(functools.partial(slot_kernel, (slots, blocks, rows, erows...  3.45 us
    pallas_call x1, Pallas kernels, image(): pl.pallas_call(image_kernel, in_specs=[pl.BlockSpec(memory_space=pltpu.SM...  3.25 us
  transfers between devices with their start and end apart: 9, of which 8 were waited for; matrix products, arithmetic and copies ran while one was open for 0% of the time, Pallas kernels for 0%

profile of v1, /device:TPU:1, one launch (start us, length us, event | category | flops | bytes accessed | tf_op | source)
XLA Modules:
  0.0 84.8 jit_solution(1682095293408448163)
XLA Ops:
  0.0 0.8 copy.15
  0.8 0.1 reshape.18.foot
  0.9 1.9 %copy-done.8 = bf16[6,512,512]{2,1,0:T(8,128)(2,1)S(1)} copy-done((bf16[6,512,512]{2,1,0:T(8,128)(2,1)S(1)}, bf16[6,512,512]{2,1,0:T(8,128)(2,1)}, u32[]{:S(2)}) %copy-start.8) | copy-done | bytes 3145752
  2.7 1.1 %copy-done.9 = bf16[6,128,512]{2,1,0:T(8,128)(2,1)S(1)} copy-done((bf16[6,128,512]{2,1,0:T(8,128)(2,1)S(1)}, bf16[6,128,512]{2,1,0:T(8,128)(2,1)}, u32[]{:S(2)}) %copy-start.9) | copy-done | bytes 786456
  3.9 3.5 %slot_terms.1 = (f32[2,4,128,128]{3,2,1,0:T(8,128)S(1)}, f32[2,4,384,128]{3,2,1,0:T(8,128)S(1)}, f32[2,4,128,128]{3,2,1,0:T(8,128)S(1)}) custom-call(s32[24]{0:T(128)S(1)} %reshape.18.foot, bf16[12,4096,128]{2,1,0:T(8,128)(2,1)} %bitcast.50, bf16[6,512,512]{2,1,0:T(8,128)(2,1)S(1)} %copy-done.8, bf16[6,128,512]{2,1,0:T(8,128)(2,1)S(1)} %copy-done.9), custom_call_target="tpu_custom_call" | custom-call | flops 8053063680 | bytes 12582912 | tf_op jit(solution)/shard_map/slot_terms/pallas_call | solution.py:97
  7.3 4.9 %collective-permute-start = (f32[2,4,128,128]{3,2,1,0:T(8,128)S(1)}, f32[2,4,128,128]{3,2,1,0:T(8,128)S(1)}, u32[]{:S(2)}, u32[]{:S(2)}) collective-permute-start(f32[2,4,128,128]{3,2,1,0:T(8,128)S(1)} %get-tuple-element.9), channel_id=1, source_target_pairs={{0,1},{1,2},{2,3},{3,4},{4,5},{5,6},{6,7},{7,8},{8,9},{9,10},{10,1... | collective-permute-start | bytes 1572872 | tf_op jit(solution)/shard_map/ppermute | solution.py:264
  12.3 2.6 %collective-permute-start.4 = (f32[2,384,128]{2,1,0:T(8,128)S(1)}, f32[2,384,128]{2,1,0:T(8,128)S(1)}, u32[]{:S(2)}, u32[]{:S(2)}) collective-permute-start(f32[2,384,128]{2,1,0:T(8,128)S(1)} %get-tuple-element.13), channel_id=1, source_target_pairs={{0,192},{64,128},{128,64},{192,0},{1,193},{65,129},{129,65},{193,1... | collective-permute-start | bytes 1179656 | tf_op jit(solution)/shard_map/ppermute | solution.py:258
  14.9 3.5 %collective-permute-done = f32[2,4,128,128]{3,2,1,0:T(8,128)S(1)} collective-permute-done((f32[2,4,128,128]{3,2,1,0:T(8,128)S(1)}, f32[2,4,128,128]{3,2,1,0:T(8,128)S(1)}, u32[]{:S(2)}, u32[]{:S(2)}) %collective-permute-start) | collective-permute-done | bytes 524320 | tf_op jit(solution)/shard_map/ppermute | solution.py:264
  18.5 2.6 %collective-permute-start.2 = (f32[2,128,128]{2,1,0:T(8,128)S(1)}, f32[2,128,128]{2,1,0:T(8,128)S(1)}, u32[]{:S(2)}, u32[]{:S(2)}) collective-permute-start(f32[2,128,128]{2,1,0:T(8,128)S(1)} %get-tuple-element.17), channel_id=1, source_target_pairs={{0,192},{64,128},{128,64},{192,0},{1,193},{65,129},{129,65},{193,1... | collective-permute-start | bytes 393224 | tf_op jit(solution)/shard_map/ppermute | solution.py:258
  21.0 2.8 %collective-permute-done.4.hb = f32[2,384,128]{2,1,0:T(8,128)S(1)} collective-permute-done((f32[2,384,128]{2,1,0:T(8,128)S(1)}, f32[2,384,128]{2,1,0:T(8,128)S(1)}, u32[]{:S(2)}, u32[]{:S(2)}) %collective-permute-start.4) | collective-permute-done | bytes 393248 | tf_op jit(solution)/shard_map/ppermute | solution.py:258
  23.8 2.2 %collective-permute-done.3.ha = f32[2,384,128]{2,1,0:T(8,128)S(1)} collective-permute-done((f32[2,384,128]{2,1,0:T(8,128)S(1)}, f32[2,384,128]{2,1,0:T(8,128)S(1)}, u32[]{:S(2)}, u32[]{:S(2)}) %collective-permute-start.3) | collective-permute-done | bytes 393248 | tf_op jit(solution)/shard_map/ppermute | solution.py:258
  26.0 0.1 fusion
  26.1 0.1 collective-permute-start.8
  26.2 1.3 %collective-permute-start.7 = (f32[384,128]{1,0:T(8,128)S(1)}, f32[384,128]{1,0:T(8,128)S(1)}, u32[]{:S(2)}, u32[]{:S(2)}) collective-permute-start(f32[384,128]{1,0:T(8,128)S(1)} %get-tuple-element.12), channel_id=1, source_target_pairs={{0,192},{64,128},{128,64},{192,0},{1,193},{65,129},{129,65},{193,1... | collective-permute-start | bytes 589832 | tf_op jit(solution)/shard_map/ppermute | solution.py:258
  27.5 0.3 collective-permute-done.1.la
  27.9 0.5 collective-permute-start.6
  28.5 1.5 %collective-permute-start.5 = (f32[128,128]{1,0:T(8,128)S(1)}, f32[128,128]{1,0:T(8,128)}, u32[]{:S(2)}, u32[]{:S(2)}) collective-permute-start(f32[128,128]{1,0:T(8,128)S(1)} %get-tuple-element.16), channel_id=1, source_target_pairs={{0,192},{64,128},{128,64},{192,0},{1,193},{65,129},{129,65},{193,1... | collective-permute-start | bytes 196616 | tf_op jit(solution)/shard_map/ppermute | solution.py:258
  30.0 2.1 %collective-permute-done.8.hqb = f32[384,128]{1,0:T(8,128)S(1)} collective-permute-done((f32[384,128]{1,0:T(8,128)S(1)}, f32[384,128]{1,0:T(8,128)S(1)}, u32[]{:S(2)}, u32[]{:S(2)}) %collective-permute-start.8) | collective-permute-done | bytes 196640 | tf_op jit(solution)/shard_map/ppermute | solution.py:258
  32.1 0.6 collective-permute-done.7.hqa
  32.7 0.8 collective-permute-done.6.lqb
  33.5 0.6 collective-permute-done.5.lqa
  34.2 3.0 %pack.1 = f32[1024,128]{1,0:T(8,128)} custom-call(f32[2,4,128,128]{3,2,1,0:T(8,128)} %copy-done.10, f32[2,4,384,128]{3,2,1,0:T(8,128)} %copy-done, f32[2,128,128]{2,1,0:T(8,128)} %copy-done.14, f32[2,128,128]{2,1,0:T(8,128)} %copy-done.13, f32[2,384,128]{2,1,0:T(8,128)} %copy-done.12, f32[2,384,128]{2,1,0:T(8,128)} %copy-done.11, ...), custom_call_target="tpu_custom_call" | custom-call | tf_op jit(solution)/shard_map/pack/pallas_call | solution.py:131
  37.2 44.3 %all_to_all.5 = f32[64,16,128]{2,1,0:T(8,128)S(1)} all-to-all(f32[64,16,128]{2,1,0:T(8,128)} %bitcast.49), channel_id=1, replica_groups=mesh['aperture'=4,'tile'=64] {'tile'}, dimensions={0} | all-to-all | bytes 1048576 | tf_op jit(solution)/shard_map/all_to_all | solution.py:271
  81.5 3.3 %image.1 = f32[2,512,128]{2,1,0:T(8,128)} custom-call(s32[2,2]{1,0:T(2,128)S(1)} %copy-done.7, f32[1024,128]{1,0:T(8,128)S(1)} %bitcast.48, bf16[256,256]{1,0:T(8,128)(2,1)S(1)} %copy-done.6, bf16[256,256]{1,0:T(8,128)(2,1)S(1)} %copy-done.5, bf16[512,512]{1,0:T(8,128)(2,1)S(1)} %copy-done.2, bf16[512,512]{1,0:T(8,128)(2,1)S(1)} %copy-done.1, ...), custom_call_target="tpu_custom_call" | custom-call | tf_op jit(solution)/shard_map/image/pallas_call | solution.py:245
  (39 shorter events, 0.2 us)
Async XLA Ops:
  0.9 1.9 %copy-start.8 = (bf16[6,512,512]{2,1,0:T(8,128)(2,1)S(1)}, bf16[6,512,512]{2,1,0:T(8,128)(2,1)}, u32[]{:S(2)}) copy-start(bf16[6,512,512]{2,1,0:T(8,128)(2,1)} %own_hbm.1) | copy-start | bytes 9437188
  7.3 18.7 %copy-start = (f32[2,4,384,128]{3,2,1,0:T(8,128)}, f32[2,4,384,128]{3,2,1,0:T(8,128)S(1)}, u32[]{:S(2)}) copy-start(f32[2,4,384,128]{3,2,1,0:T(8,128)S(1)} %get-tuple-element.10.high_ref) | copy-start | bytes 4718596
  7.3 11.0 %collective-permute-start = (f32[2,4,128,128]{3,2,1,0:T(8,128)S(1)}, f32[2,4,128,128]{3,2,1,0:T(8,128)S(1)}, u32[]{:S(2)}, u32[]{:S(2)}) collective-permute-start(f32[2,4,128,128]{3,2,1,0:T(8,128)S(1)} %get-tuple-element.9), channel_id=1, source_target_pairs={{0,1},{1,2},{2,3},{3,4},{4,5},{5,6},{6,7},{7,8},{8,9},{9,10},{10,1... | collective-permute-start | bytes 1572872 | tf_op jit(solution)/shard_map/ppermute | solution.py:264
  12.3 11.5 %collective-permute-start.4 = (f32[2,384,128]{2,1,0:T(8,128)S(1)}, f32[2,384,128]{2,1,0:T(8,128)S(1)}, u32[]{:S(2)}, u32[]{:S(2)}) collective-permute-start(f32[2,384,128]{2,1,0:T(8,128)S(1)} %get-tuple-element.13), channel_id=1, source_target_pairs={{0,192},{64,128},{128,64},{192,0},{1,193},{65,129},{129,65},{193,1... | collective-permute-start | bytes 1179656 | tf_op jit(solution)/shard_map/ppermute | solution.py:258
  14.9 11.1 %collective-permute-start.3 = (f32[2,384,128]{2,1,0:T(8,128)S(1)}, f32[2,384,128]{2,1,0:T(8,128)S(1)}, u32[]{:S(2)}, u32[]{:S(2)}) collective-permute-start(f32[2,384,128]{2,1,0:T(8,128)S(1)} %get-tuple-element.14), channel_id=1, source_target_pairs={{0,64},{64,0},{128,192},{192,128},{1,65},{65,1},{129,193},{193,129... | collective-permute-start | bytes 1179656 | tf_op jit(solution)/shard_map/ppermute | solution.py:258
  18.4 15.7 %copy-start.10 = (f32[2,4,128,128]{3,2,1,0:T(8,128)}, f32[2,4,128,128]{3,2,1,0:T(8,128)S(1)}, u32[]{:S(2)}) copy-start(f32[2,4,128,128]{3,2,1,0:T(8,128)S(1)} %add.15.low_ref) | copy-start | bytes 1572868
  18.5 9.0 %collective-permute-start.2 = (f32[2,128,128]{2,1,0:T(8,128)S(1)}, f32[2,128,128]{2,1,0:T(8,128)S(1)}, u32[]{:S(2)}, u32[]{:S(2)}) collective-permute-start(f32[2,128,128]{2,1,0:T(8,128)S(1)} %get-tuple-element.17), channel_id=1, source_target_pairs={{0,192},{64,128},{128,64},{192,0},{1,193},{65,129},{129,65},{193,1... | collective-permute-start | bytes 393224 | tf_op jit(solution)/shard_map/ppermute | solution.py:258
  21.0 6.8 %collective-permute-start.1 = (f32[2,128,128]{2,1,0:T(8,128)S(1)}, f32[2,128,128]{2,1,0:T(8,128)S(1)}, u32[]{:S(2)}, u32[]{:S(2)}) collective-permute-start(f32[2,128,128]{2,1,0:T(8,128)S(1)} %get-tuple-element.18), channel_id=1, source_target_pairs={{0,64},{64,0},{128,192},{192,128},{1,65},{65,1},{129,193},{193,129... | collective-permute-start | bytes 393224 | tf_op jit(solution)/shard_map/ppermute | solution.py:258
  23.8 10.3 %copy-start.11 = (f32[2,384,128]{2,1,0:T(8,128)}, f32[2,384,128]{2,1,0:T(8,128)S(1)}, u32[]{:S(2)}) copy-start(f32[2,384,128]{2,1,0:T(8,128)S(1)} %collective-permute-done.4.hb) | copy-start | bytes 1179652
  26.0 8.1 %copy-start.12 = (f32[2,384,128]{2,1,0:T(8,128)}, f32[2,384,128]{2,1,0:T(8,128)S(1)}, u32[]{:S(2)}) copy-start(f32[2,384,128]{2,1,0:T(8,128)S(1)} %collective-permute-done.3.ha) | copy-start | bytes 1179652
  26.1 6.0 %collective-permute-start.8 = (f32[384,128]{1,0:T(8,128)S(1)}, f32[384,128]{1,0:T(8,128)S(1)}, u32[]{:S(2)}, u32[]{:S(2)}) collective-permute-start(f32[384,128]{1,0:T(8,128)S(1)} %get-tuple-element.11), channel_id=1, source_target_pairs={{0,64},{64,0},{128,192},{192,128},{1,65},{65,1},{129,193},{193,129... | collective-permute-start | bytes 589832 | tf_op jit(solution)/shard_map/ppermute | solution.py:258
  26.2 6.5 %collective-permute-start.7 = (f32[384,128]{1,0:T(8,128)S(1)}, f32[384,128]{1,0:T(8,128)S(1)}, u32[]{:S(2)}, u32[]{:S(2)}) collective-permute-start(f32[384,128]{1,0:T(8,128)S(1)} %get-tuple-element.12), channel_id=1, source_target_pairs={{0,192},{64,128},{128,64},{192,0},{1,193},{65,129},{129,65},{193,1... | collective-permute-start | bytes 589832 | tf_op jit(solution)/shard_map/ppermute | solution.py:258
  27.5 6.6 %copy-start.13 = (f32[2,128,128]{2,1,0:T(8,128)}, f32[2,128,128]{2,1,0:T(8,128)S(1)}, u32[]{:S(2)}) copy-start(f32[2,128,128]{2,1,0:T(8,128)S(1)} %collective-permute-done.2.lb) | copy-start | bytes 393220
  27.9 6.3 %copy-start.14 = (f32[2,128,128]{2,1,0:T(8,128)}, f32[2,128,128]{2,1,0:T(8,128)S(1)}, u32[]{:S(2)}) copy-start(f32[2,128,128]{2,1,0:T(8,128)S(1)} %collective-permute-done.1.la) | copy-start | bytes 393220
  27.9 5.6 %collective-permute-start.6 = (f32[128,128]{1,0:T(8,128)S(1)}, f32[128,128]{1,0:T(8,128)}, u32[]{:S(2)}, u32[]{:S(2)}) collective-permute-start(f32[128,128]{1,0:T(8,128)S(1)} %get-tuple-element.15), channel_id=1, source_target_pairs={{0,64},{64,0},{128,192},{192,128},{1,65},{65,1},{129,193},{193,129... | collective-permute-start | bytes 196616 | tf_op jit(solution)/shard_map/ppermute | solution.py:258
  28.4 53.1 %copy-start.1 = (bf16[512,512]{1,0:T(8,128)(2,1)S(1)}, bf16[512,512]{1,0:T(8,128)(2,1)}, u32[]{:S(2)}) copy-start(bf16[512,512]{1,0:T(8,128)(2,1)} %constant.15.clone.s_lo) | copy-start | bytes 1572868
  28.4 53.1 %copy-start.2 = (bf16[512,512]{1,0:T(8,128)(2,1)S(1)}, bf16[512,512]{1,0:T(8,128)(2,1)}, u32[]{:S(2)}) copy-start(bf16[512,512]{1,0:T(8,128)(2,1)} %constant.14.clone.s_hi) | copy-start | bytes 1572868
  28.4 53.1 %copy-start.3 = (f32[128,256]{1,0:T(8,128)S(1)}, f32[128,256]{1,0:T(8,128)}, u32[]{:S(2)}) copy-start(f32[128,256]{1,0:T(8,128)} %constant.17.clone.tw_s) | copy-start | bytes 393220
  28.4 53.1 %copy-start.4 = (f32[128,256]{1,0:T(8,128)S(1)}, f32[128,256]{1,0:T(8,128)}, u32[]{:S(2)}) copy-start(f32[128,256]{1,0:T(8,128)} %constant.16.clone.tw_c) | copy-start | bytes 393220
  28.4 53.1 %copy-start.5 = (bf16[256,256]{1,0:T(8,128)(2,1)S(1)}, bf16[256,256]{1,0:T(8,128)(2,1)}, u32[]{:S(2)}) copy-start(bf16[256,256]{1,0:T(8,128)(2,1)} %constant.13.clone.f_lo) | copy-start | bytes 393220
  28.4 53.1 %copy-start.6 = (bf16[256,256]{1,0:T(8,128)(2,1)S(1)}, bf16[256,256]{1,0:T(8,128)(2,1)}, u32[]{:S(2)}) copy-start(bf16[256,256]{1,0:T(8,128)(2,1)} %constant.12.clone.f_hi) | copy-start | bytes 393220
  28.4 53.1 %copy-start.7 = (s32[2,2]{1,0:T(2,128)S(1)}, s32[2,2]{1,0:T(2,128)}, u32[]{:S(2)}) copy-start(s32[2,2]{1,0:T(2,128)} %edges.1) | copy-start | bytes 52
  28.5 5.7 %collective-permute-start.5 = (f32[128,128]{1,0:T(8,128)S(1)}, f32[128,128]{1,0:T(8,128)}, u32[]{:S(2)}, u32[]{:S(2)}) collective-permute-start(f32[128,128]{1,0:T(8,128)S(1)} %get-tuple-element.16), channel_id=1, source_target_pairs={{0,192},{64,128},{128,64},{192,0},{1,193},{65,129},{129,65},{193,1... | collective-permute-start | bytes 196616 | tf_op jit(solution)/shard_map/ppermute | solution.py:258
  32.1 2.1 %copy-start.15 = (f32[384,128]{1,0:T(8,128)}, f32[384,128]{1,0:T(8,128)S(1)}, u32[]{:S(2)}) copy-start(f32[384,128]{1,0:T(8,128)S(1)} %collective-permute-done.8.hqb) | copy-start | bytes 589828
  (2 other events, 2.6 us)

commit v2 on v1

--- a/solution.py
+++ b/solution.py
@@ -18,113 +18,185 @@
     return pl.BlockSpec(memory_space=pltpu.VMEM)
 
 
+def aperture(foot):
+    return lax.axis_index("aperture")
+
+
 def position(part, relative):
     return (relative - 1) & 3 if part == 0 else 3 - relative
 
 
-def slot_kernel(cfg, foot, x_hbm, own_hbm, edge_hbm, low_ref, high_ref, rim_ref, xs, owns, edges, wide0, wide1, sems, bsem):
-    slots, blocks, rows, erows = cfg
-    me = lax.axis_index("aperture")
-    depth = x_hbm.shape[1] // 8
+def live(foot, slots, blocks):
     count = jnp.int32(0)
     for s in range(slots):
-        count = count + (foot[2 * s] < blocks).astype(jnp.int32)
+        count = count + (foot[0, s] < blocks).astype(jnp.int32)
+    return count
+
+
+def early_kernel(cfg, foot, x_hbm, own_hbm, edge_hbm, high_ref, rim_ref, x_ref, sums, xs, owns, edges, wide0, wide1, wide2, wide3, sems, bsem):
+    slots, blocks, begin, tall, erows = cfg
+    me = aperture(foot)
+    depth = x_hbm.shape[1] // 8
+    count = live(foot, slots, blocks)
 
     def fetch(s):
         return pltpu.make_async_copy(x_hbm.at[s], xs.at[s], sems.at[s])
 
-    own_copy = pltpu.make_async_copy(own_hbm, owns, bsem.at[0])
-    edge_copy = pltpu.make_async_copy(edge_hbm, edges, bsem.at[1])
-    fetch(0).start()
-    own_copy.start()
-    edge_copy.start()
-    for s in range(1, slots):
+    def start(s):
         @pl.when(s < count)
         def _():
             fetch(s).start()
-    low_ref[...] = jnp.zeros_like(low_ref)
-    high_ref[...] = jnp.zeros_like(high_ref)
-    rim_ref[...] = jnp.zeros_like(rim_ref)
+
+    def arrive(s):
+        @pl.when(s < count)
+        def _():
+            fetch(s).wait()
+
+    own_copy = pltpu.make_async_copy(own_hbm.at[:, pl.ds(begin, tall), :], owns.at[pl.ds(0, blocks)], bsem.at[0])
+    edge_copy = pltpu.make_async_copy(edge_hbm, edges.at[pl.ds(0, blocks)], bsem.at[1])
+    fetch(0).start()
+    start(1)
+    own_copy.start()
+    edge_copy.start()
+    for s in range(2, slots):
+        start(s)
+    owns[blocks] = jnp.zeros((tall, depth), bf16)
+    edges[blocks] = jnp.zeros((erows, depth), bf16)
+    sums[...] = jnp.zeros_like(sums)
 
     def widen(s, wide):
-        wide[...] = xs[s].astype(f32)
-
-    def multiply(s, wide):
-        e = foot[2 * s + 1]
-        keep = (e < blocks).astype(bf16)
-        kern = jnp.concatenate([owns[foot[2 * s]], edges[jnp.minimum(e, blocks - 1)] * keep], axis=0)
+        wide[...] = xs[jnp.minimum(s, count - 1)].astype(f32)
+
+    def kernels(s):
+        at = jnp.minimum(s, count - 1)
+        o, e = foot[0, at], foot[1, at]
+        own = owns[jnp.where(s < count, o, blocks)]
+        edge = edges[jnp.where(s < count, e, blocks)]
+        return jnp.concatenate([own, edge], axis=0)
+
+    def columns(p, wide):
+        return jnp.concatenate([wide[pl.ds(2 * j + p, depth, stride=8), :].astype(bf16) for j in range(4)], axis=1)
+
+    def multiply(s, first, second):
+        ka, kb = kernels(s), kernels(s + 1)
         for p in range(2):
-            x = jnp.concatenate(
-                [wide[pl.ds(2 * j + p, depth, stride=8), :].astype(bf16) for j in range(4)], axis=1
-            )
-            y = jnp.dot(kern, x, preferred_element_type=f32)
-            for d in range(4):
-                pos = position(p, me ^ d)
-                part = y[:, d * LANES:(d + 1) * LANES]
-                low_ref[p, pos] += part[:erows]
-                high_ref[p, pos] += part[erows:rows]
-                rim_ref[p, pos] += part[rows:]
+            xa, xb = columns(p, first), columns(p, second)
+            x_ref[s, p] = xa
+            x_ref[s + 1, p] = xb
+            y = jnp.dot(ka, xa, preferred_element_type=f32) + jnp.dot(kb, xb, preferred_element_type=f32)
+            sums[p] += y
 
     fetch(0).wait()
     widen(0, wide0)
+    arrive(1)
+    widen(1, wide1)
     own_copy.wait()
     edge_copy.wait()
 
     def step(s, here, there):
-        @pl.when(s + 1 < count)
+        arrive(s + 2)
+        arrive(s + 3)
+        widen(s + 2, there[0])
+        widen(s + 3, there[1])
+        multiply(s, *here)
+
+    def quad(t, carry):
+        step(4 * t, (wide0, wide1), (wide2, wide3))
+
+        @pl.when(4 * t + 2 < count)
         def _():
-            fetch(s + 1).wait()
-        widen(jnp.minimum(s + 1, count - 1), there)
-        multiply(s, here)
-
-    def pair(t, carry):
-        step(2 * t, wide0, wide1)
-
-        @pl.when(2 * t + 1 < count)
-        def _():
-            step(2 * t + 1, wide1, wide0)
+            step(4 * t + 2, (wide2, wide3), (wide0, wide1))
         return carry
-    lax.fori_loop(0, (count + 1) // 2, pair, 0)
-
-
-def slot_terms(sectors, foot, own, edge):
+    lax.fori_loop(0, (count + 3) // 4, quad, 0)
+    for p in range(2):
+        for j in range(4):
+            pos = position(p, me ^ j)
+            high_ref[p, pos] = sums[p, :tall, j * LANES:(j + 1) * LANES]
+            rim_ref[p, pos] = sums[p, tall:, j * LANES:(j + 1) * LANES]
+
+
+def early_terms(sectors, foot, own, edge, begin):
     slots, depth, parts, lines = sectors.shape
     blocks, rows, _ = own.shape
-    erows = edge.shape[1]
+    tall, erows = rows - begin, edge.shape[1]
     quarter = lines // 4
     sectors = sectors.reshape(slots, depth, 2, 4, LANES).transpose(0, 1, 3, 2, 4).reshape(slots, depth * 8, LANES)
     hbm = pl.BlockSpec(memory_space=pltpu.HBM)
     return pl.pallas_call(
-        functools.partial(slot_kernel, (slots, blocks, rows, erows)),
+        functools.partial(early_kernel, (slots, blocks, begin, tall, erows)),
         in_specs=[pl.BlockSpec(memory_space=pltpu.SMEM), hbm, hbm, hbm],
         out_specs=[vmem()] * 3,
-        out_shape=[jax.ShapeDtypeStruct((2, 4, r, quarter), f32) for r in (erows, rows - erows, erows)],
+        out_shape=[jax.ShapeDtypeStruct((2, 4, r, quarter), f32) for r in (tall, erows)]
+        + [jax.ShapeDtypeStruct((slots, 2, depth, lines), bf16)],
         scratch_shapes=[
+            pltpu.VMEM((2, tall + erows, lines), f32),
             pltpu.VMEM((slots, depth * 8, LANES), bf16),
-            pltpu.VMEM((blocks, rows, depth), bf16),
-            pltpu.VMEM((blocks, erows, depth), bf16),
-            pltpu.VMEM((depth * 8, LANES), f32),
-            pltpu.VMEM((depth * 8, LANES), f32),
+            pltpu.VMEM((blocks + 1, tall, depth), bf16),
+            pltpu.VMEM((blocks + 1, erows, depth), bf16),
+            *[pltpu.VMEM((depth * 8, LANES), f32)] * 4,
             pltpu.SemaphoreType.DMA((slots,)),
             pltpu.SemaphoreType.DMA((2,)),
         ],
-        compiler_params=pltpu.CompilerParams(vmem_limit_bytes=40 << 20),
+        compiler_params=pltpu.CompilerParams(vmem_limit_bytes=36 << 20),
         cost_estimate=pl.CostEstimate(
-            flops=4 * slots * depth * lines * (rows + erows), bytes_accessed=slots * depth * lines * 4, transcendentals=0
+            flops=4 * slots * depth * lines * (tall + erows), bytes_accessed=slots * depth * lines * 4, transcendentals=0
         ),
-        name="slot_terms",
-    )(foot, sectors, own, edge)
-
-
-def pack_kernel(low_ref, high_ref, la, lb, ha, hb, lqa, lqb, hqa, hqb, out_ref):
-    erows = low_ref.shape[2]
-    for p, (lr, hr, lq, hq) in enumerate(((la, ha, lqa, hqa), (lb, hb, lqb, hqb))):
-        low = low_ref[p, 3] + lr[0] + lq[...]
-        out_ref[pl.ds(4 * p, LANES, stride=8), :] = low.T
-        for j in range(high_ref.shape[2] // LANES):
-            at = pl.ds(j * LANES, LANES)
-            high = high_ref[p, 3, at] + hr[0, at] + hq[at]
-            out_ref[pl.ds(4 * p + 1 + j, LANES, stride=8), :] = high.T
+        name="early_terms",
+    )(foot, *[pltpu.with_memory_space_constraint(v, pltpu.HBM) for v in (sectors, own, edge)])
+
+
+def late_kernel(cfg, foot, x_ref, own_ref, low_ref, sums):
+    slots, blocks, tall = cfg
+    me = aperture(foot)
+    count = live(foot, slots, blocks)
+    sums[...] = jnp.zeros_like(sums)
+
+    def add(s, ops):
+        for p in range(2):
+            y = sum(jnp.dot(own_ref[foot[0, s + i], :tall], x_ref[s + i, p], preferred_element_type=f32) for i in ops)
+            sums[p] += y
+
+    def pair(t, carry):
+        add(2 * t, (0, 1))
+        return carry
+    lax.fori_loop(0, count // 2, pair, 0)
+
+    @pl.when(count % 2 == 1)
+    def _():
+        add(count - 1, (0,))
+    for p in range(2):
+        for j in range(4):
+            low_ref[p, position(p, me ^ j)] = sums[p, :, j * LANES:(j + 1) * LANES]
+
+
+def late_terms(x, foot, own, tall):
+    slots, parts, depth, lines = x.shape
+    blocks = own.shape[0]
+    return pl.pallas_call(
+        functools.partial(late_kernel, (slots, blocks, tall)),
+        in_specs=[pl.BlockSpec(memory_space=pltpu.SMEM), vmem(), vmem()],
+        out_specs=vmem(),
+        out_shape=jax.ShapeDtypeStruct((2, 4, tall, lines // 4), f32),
+        scratch_shapes=[pltpu.VMEM((2, tall, lines), f32)],
+        compiler_params=pltpu.CompilerParams(vmem_limit_bytes=24 << 20),
+        cost_estimate=pl.CostEstimate(
+            flops=4 * slots * depth * lines * tall, bytes_accessed=slots * depth * lines * 4, transcendentals=0
+        ),
+        name="late_terms",
+    )(foot, x, own)
+
+
+def pack_kernel(*refs):
+    *terms, out_ref = refs
+    for p in range(2):
+        keeps, firsts, second = terms[5 * p:5 * p + 2], terms[5 * p + 2:5 * p + 4], terms[5 * p + 4]
+        row = 0
+        for keep, first in zip(keeps, firsts):
+            for j in range(keep.shape[0] // LANES):
+                at = pl.ds(j * LANES, LANES)
+                total = keep[at] + first[at] + second[pl.ds(row * LANES, LANES)]
+                out_ref[pl.ds(4 * p + row, LANES, stride=8), :] = total.T
+                row += 1
 
 
 def pack(*args):
@@ -133,6 +205,7 @@
         in_specs=[vmem()] * len(args),
         out_specs=vmem(),
         out_shape=jax.ShapeDtypeStruct((8 * LANES, LANES), f32),
+        compiler_params=pltpu.CompilerParams(vmem_limit_bytes=8 << 20),
         name="pack",
     )(*args)
 
@@ -248,7 +321,7 @@
         out_specs=vmem(),
         out_shape=jax.ShapeDtypeStruct((2, 2 * inner, LANES), f32),
         scratch_shapes=[pltpu.VMEM((2 * inner, 2 * LANES), f32)],
-        compiler_params=pltpu.CompilerParams(vmem_limit_bytes=24 << 20),
+        compiler_params=pltpu.CompilerParams(vmem_limit_bytes=12 << 20),
         name="image",
     )(edges, x, *consts)
     return out.reshape(2, inner, 2, LANES).transpose(0, 2, 1, 3).reshape(2, 2, width)
@@ -260,14 +333,17 @@
 
 def on_device(sectors, footprint, own_blocks, edge_blocks, edges):
     tiles = lax.axis_size("tile")
-    low, high, rim = slot_terms(sectors[0], footprint.reshape(-1), own_blocks, edge_blocks)
+    foot = footprint[0].T
+    half = own_blocks.shape[1] // 2
+    high, rim, spread = early_terms(sectors[0], foot, own_blocks, edge_blocks, half)
     incoming = lax.ppermute(rim, "tile", [(i, i + 1) for i in range(tiles - 1)])
     ha, hb = swap(high[0, :2], 1), swap(high[1, :2], 3)
-    low = low + incoming
+    low = late_terms(spread, foot, own_blocks, half)
+    low = low + jnp.pad(incoming, ((0, 0), (0, 0), (0, half - incoming.shape[2]), (0, 0)))
     la, lb = swap(low[0, :2], 1), swap(low[1, :2], 3)
-    hqa, hqb = swap(high[0, 2] + ha[1], 3), swap(high[1, 2] + hb[1], 1)
-    lqa, lqb = swap(low[0, 2] + la[1], 3), swap(low[1, 2] + lb[1], 1)
-    packed = pack(low, high, la, lb, ha, hb, lqa, lqb, hqa, hqb)
+    qa = swap(jnp.concatenate([low[0, 2] + la[1], high[0, 2] + ha[1]]), 3)
+    qb = swap(jnp.concatenate([low[1, 2] + lb[1], high[1, 2] + hb[1]]), 1)
+    packed = pack(low[0, 3], high[0, 3], la[0], ha[0], qa, low[1, 3], high[1, 3], lb[0], hb[0], qb)
     moved = lax.all_to_all(packed.reshape(tiles, 16, LANES), "tile", 0, 0, tiled=True)
     return image(edges, moved.reshape(tiles * 16, LANES), tiles * own_blocks.shape[1])
 

time: 85.3 us -> 78.3 us (0.918); the launches traced: 84.8 us -> 79.5 us
  blocking collectives: 44.3 us -> 32.1 us
  waiting for transfers between devices: 12.9 us -> 18.1 us
  starting transfers between devices: 13.5 us -> 18.5 us
  local copies, waits for them, and re-layouts: 4.01 us -> 1.03 us
    all_to_all x1, blocking collectives: 44.3 us -> 32.1 us  [on_device(): lax.all_to_all(packed.reshape(tiles, 16, LANES), 'tile', 0, 0, tiled=True)]
    ppermute x8 -> x6, waiting for transfers between devices: 9.47 us -> 17.7 us  [swap(): return lax.ppermute(block, 'aperture', [(i, i ^ flip) for i in range(4)])]
    ppermute x8 -> x6, starting transfers between devices: 8.58 us -> 16.6 us  [swap(): return lax.ppermute(block, 'aperture', [(i, i ^ flip) for i in range(4)])]
    ppermute x1, waiting for transfers between devices: 3.48 us -> 0.36 us  [on_device(): incoming = lax.ppermute(rim, 'tile', [(i, i + 1) for i in range(tiles - 1)])]
    ppermute x1, starting transfers between devices: 4.92 us -> 1.91 us  [on_device(): incoming = lax.ppermute(rim, 'tile', [(i, i + 1) for i in range(tiles - 1)])]
    unnamed x35 -> x18, local copies, waits for them, and re-layouts: 3.85 us -> 0.88 us
    pallas_call x1, Pallas kernels: 2.98 us -> 0.2 us  [pack(): pl.pallas_call(pack_kernel, in_specs=[vmem()] * len(args), out_specs=vmem...]
    pallas_call x1 -> x2, Pallas kernels: 3.45 us -> 5.83 us  [the longest x1 4.41 us: early_terms(): pl.pallas_call(functools.partial(early_kernel, (slots, blocks, begin, tal...]
  transfers between devices with their start and end apart: 9 -> 7, of which waited for: 8 -> 5; matrix products, arithmetic and copies ran while one was open for 0% -> 0% of each run, Pallas kernels for 0% -> 2%
where the time goes in v2:
time: 78.3 us; the launch traced here: 79.5 us
  blocking collectives  32.1 us (41%)
  starting transfers between devices  18.5 us (24%)
  waiting for transfers between devices  18.1 us (23%)
  Pallas kernels  9.37 us (12%)
  local copies, waits for them, and re-layouts  1.03 us (1%)
    all_to_all x1, blocking collectives, on_device(): lax.all_to_all(packed.reshape(tiles, 16, LANES), 'tile', 0, 0, tiled=True)  32.1 us
    ppermute x6, waiting for transfers between devices, swap(): return lax.ppermute(block, 'aperture', [(i, i ^ flip) for i in range(4)])  17.7 us
    ppermute x6, starting transfers between devices, swap(): return lax.ppermute(block, 'aperture', [(i, i ^ flip) for i in range(4)])  16.6 us
    pallas_call x1, Pallas kernels, early_terms(): pl.pallas_call(functools.partial(early_kernel, (slots, blocks, begin, tal...  4.41 us
    pallas_call x1, Pallas kernels, image(): pl.pallas_call(image_kernel, in_specs=[pl.BlockSpec(memory_space=pltpu.SM...  3.34 us
    ppermute x1, starting transfers between devices, on_device(): incoming = lax.ppermute(rim, 'tile', [(i, i + 1) for i in range(tiles - 1)])  1.91 us
  transfers between devices with their start and end apart: 7, of which 5 were waited for; matrix products, arithmetic and copies ran while one was open for 0% of the time, Pallas kernels for 2%

profile of v2, /device:TPU:1, one launch (start us, length us, event | category | flops | bytes accessed | tf_op | source)
XLA Modules:
  0.0 79.5 jit_solution(14895320870388535943)
XLA Ops:
  0.0 0.8 %copy-done.7 = s32[1,12,2]{1,2,0:T(2,128)S(1)} copy-done((s32[1,12,2]{1,2,0:T(2,128)S(1)}, s32[1,12,2]{1,2,0:T(2,128)}, u32[]{:S(2)}) %copy-start.7) | copy-done | bytes 120
  0.8 4.4 %early_terms.1 = (f32[2,4,256,128]{3,2,1,0:T(8,128)S(1)}, f32[2,4,128,128]{3,2,1,0:T(8,128)S(1)}, bf16[12,2,512,512]{3,2,1,0:T(8,128)(2,1)S(1)}) custom-call(s32[2,12]{1,0:T(2,128)S(1)} %bitcast.69, bf16[12,4096,128]{2,1,0:T(8,128)(2,1)} %bitcast.71, bf16[6,512,512]{2,1,0:T(8,128)(2,1)} %own_ref.1, bf16[6,128,512]{2,1,0:T(8,128)(2,1)} %edge_hbm.1), custom_call_target="tpu_custom_call" | custom-call | flops 4831838208 | bytes 12582912 | tf_op jit(solution)/shard_map/early_terms/pallas_call | solution.py:125
  5.3 12.7 %collective-permute-start.5 = (f32[2,256,128]{2,1,0:T(8,128)S(1)}, f32[2,256,128]{2,1,0:T(8,128)S(1)}, u32[]{:S(2)}, u32[]{:S(2)}) collective-permute-start(f32[2,256,128]{2,1,0:T(8,128)S(1)} %get-tuple-element.15), channel_id=1, source_target_pairs={{0,192},{64,128},{128,64},{192,0},{1,193},{65,129},{129,65},{193,1... | collective-permute-start | bytes 786440 | tf_op jit(solution)/shard_map/ppermute | solution.py:331
  18.0 1.9 %collective-permute-start = (f32[2,4,128,128]{3,2,1,0:T(8,128)S(1)}, f32[2,4,128,128]{3,2,1,0:T(8,128)S(1)}, u32[]{:S(2)}, u32[]{:S(2)}) collective-permute-start(f32[2,4,128,128]{3,2,1,0:T(8,128)S(1)} %get-tuple-element.9), channel_id=1, source_target_pairs={{0,1},{1,2},{2,3},{3,4},{4,5},{5,6},{6,7},{7,8},{8,9},{9,10},{10,1... | collective-permute-start | bytes 1572872 | tf_op jit(solution)/shard_map/ppermute | solution.py:339
  19.9 0.0 copy-start.1
  19.9 0.0 copy-start.2
  19.9 0.0 copy-start.3
  20.0 0.0 copy-start.4
  20.0 0.0 copy-start.5
  20.0 0.0 copy-start.6
  20.0 1.4 %late_terms.1 = f32[2,4,256,128]{3,2,1,0:T(8,128)S(1)} custom-call(s32[2,12]{1,0:T(2,128)S(1)} %bitcast.70, bf16[12,2,512,512]{3,2,1,0:T(8,128)(2,1)S(1)} %get-tuple-element.8.x_ref, bf16[6,512,512]{2,1,0:T(8,128)(2,1)S(1)} %copy-done), custom_call_target="tpu_custom_call" | custom-call | flops 3221225472 | bytes 12582912 | tf_op jit(solution)/shard_map/late_terms/pallas_call | solution.py:175
  21.5 0.3 collective-permute-done.5
  21.8 3.9 %collective-permute-done.2 = f32[2,256,128]{2,1,0:T(8,128)S(1)} collective-permute-done((f32[2,256,128]{2,1,0:T(8,128)S(1)}, f32[2,256,128]{2,1,0:T(8,128)S(1)}, u32[]{:S(2)}, u32[]{:S(2)}) %collective-permute-start.2) | collective-permute-done | bytes 262176 | tf_op jit(solution)/shard_map/ppermute | solution.py:331
  25.6 0.4 collective-permute-done
  26.0 0.1 pad_add_fusion
  26.1 0.4 collective-permute-start.4
  26.5 1.3 %collective-permute-start.1 = (f32[2,256,128]{2,1,0:T(8,128)S(1)}, f32[2,256,128]{2,1,0:T(8,128)S(1)}, u32[]{:S(2)}, u32[]{:S(2)}) collective-permute-start(f32[2,256,128]{2,1,0:T(8,128)S(1)} %get-tuple-element.18), channel_id=1, source_target_pairs={{0,64},{64,0},{128,192},{192,128},{1,65},{65,1},{129,193},{193,129... | collective-permute-start | bytes 786440 | tf_op jit(solution)/shard_map/ppermute | solution.py:331
  27.8 7.5 %collective-permute-done.4 = f32[2,256,128]{2,1,0:T(8,128)S(1)} collective-permute-done((f32[2,256,128]{2,1,0:T(8,128)S(1)}, f32[2,256,128]{2,1,0:T(8,128)S(1)}, u32[]{:S(2)}, u32[]{:S(2)}) %collective-permute-start.4) | collective-permute-done | bytes 262176 | tf_op jit(solution)/shard_map/ppermute | solution.py:331
  35.4 1.3 %collective-permute-start.3 = (f32[512,128]{1,0:T(8,128)S(1)}, f32[512,128]{1,0:T(8,128)S(1)}, u32[]{:S(2)}, u32[]{:S(2)}) collective-permute-start(f32[512,128]{1,0:T(8,128)S(1)} %pad_maximum_fusion), channel_id=1, source_target_pairs={{0,192},{64,128},{128,64},{192,0},{1,193},{65,129},{129,65},{193,1... | collective-permute-start | bytes 786440 | tf_op jit(solution)/shard_map/ppermute | solution.py:331
  36.7 1.0 %collective-permute-start.6 = (f32[512,128]{1,0:T(8,128)S(1)}, f32[512,128]{1,0:T(8,128)S(1)}, u32[]{:S(2)}, u32[]{:S(2)}) collective-permute-start(f32[512,128]{1,0:T(8,128)S(1)} %pad_maximum_fusion.1), channel_id=1, source_target_pairs={{0,64},{64,0},{128,192},{192,128},{1,65},{65,1},{129,193},{193,129... | collective-permute-start | bytes 786440 | tf_op jit(solution)/shard_map/ppermute | solution.py:331
  37.8 6.1 %collective-permute-done.3.refs_4_ = f32[512,128]{1,0:T(8,128)S(1)} collective-permute-done((f32[512,128]{1,0:T(8,128)S(1)}, f32[512,128]{1,0:T(8,128)S(1)}, u32[]{:S(2)}, u32[]{:S(2)}) %collective-permute-start.3) | collective-permute-done | bytes 262176 | tf_op jit(solution)/shard_map/ppermute | solution.py:331
  43.8 0.2 pack.1
  44.0 32.1 %all_to_all.5 = f32[64,16,128]{2,1,0:T(8,128)S(1)} all-to-all(f32[64,16,128]{2,1,0:T(8,128)S(1)} %bitcast.68), channel_id=1, replica_groups=mesh['aperture'=4,'tile'=64] {'tile'}, dimensions={0} | all-to-all | bytes 1048576 | tf_op jit(solution)/shard_map/all_to_all | solution.py:347
  76.1 3.3 %image.1 = f32[2,512,128]{2,1,0:T(8,128)} custom-call(s32[2,2]{1,0:T(2,128)S(1)} %copy-done.8, f32[1024,128]{1,0:T(8,128)S(1)} %bitcast.67, bf16[256,256]{1,0:T(8,128)(2,1)S(1)} %copy-done.6, bf16[256,256]{1,0:T(8,128)(2,1)S(1)} %copy-done.5, bf16[512,512]{1,0:T(8,128)(2,1)S(1)} %copy-done.2, bf16[512,512]{1,0:T(8,128)(2,1)S(1)} %copy-done.1, ...), custom_call_target="tpu_custom_call" | custom-call | tf_op jit(solution)/shard_map/image/pallas_call | solution.py:318
  (26 shorter events, 0.3 us)
Async XLA Ops:
  0.0 19.9 %copy-start = (bf16[6,512,512]{2,1,0:T(8,128)(2,1)S(1)}, bf16[6,512,512]{2,1,0:T(8,128)(2,1)}, u32[]{:S(2)}) copy-start(bf16[6,512,512]{2,1,0:T(8,128)(2,1)} %own_ref.1) | copy-start | bytes 9437188
  0.0 0.8 %copy-start.7 = (s32[1,12,2]{1,2,0:T(2,128)S(1)}, s32[1,12,2]{1,2,0:T(2,128)}, u32[]{:S(2)}) copy-start(s32[1,12,2]{1,2,0:T(2,128)} %param.12) | copy-start | bytes 292
  5.3 16.5 %collective-permute-start.5 = (f32[2,256,128]{2,1,0:T(8,128)S(1)}, f32[2,256,128]{2,1,0:T(8,128)S(1)}, u32[]{:S(2)}, u32[]{:S(2)}) collective-permute-start(f32[2,256,128]{2,1,0:T(8,128)S(1)} %get-tuple-element.15), channel_id=1, source_target_pairs={{0,192},{64,128},{128,64},{192,0},{1,193},{65,129},{129,65},{193,1... | collective-permute-start | bytes 786440 | tf_op jit(solution)/shard_map/ppermute | solution.py:331
  18.0 7.6 %collective-permute-start.2 = (f32[2,256,128]{2,1,0:T(8,128)S(1)}, f32[2,256,128]{2,1,0:T(8,128)S(1)}, u32[]{:S(2)}, u32[]{:S(2)}) collective-permute-start(f32[2,256,128]{2,1,0:T(8,128)S(1)} %get-tuple-element.16), channel_id=1, source_target_pairs={{0,64},{64,0},{128,192},{192,128},{1,65},{65,1},{129,193},{193,129... | collective-permute-start | bytes 786440 | tf_op jit(solution)/shard_map/ppermute | solution.py:331
  18.0 8.0 %collective-permute-start = (f32[2,4,128,128]{3,2,1,0:T(8,128)S(1)}, f32[2,4,128,128]{3,2,1,0:T(8,128)S(1)}, u32[]{:S(2)}, u32[]{:S(2)}) collective-permute-start(f32[2,4,128,128]{3,2,1,0:T(8,128)S(1)} %get-tuple-element.9), channel_id=1, source_target_pairs={{0,1},{1,2},{2,3},{3,4},{4,5},{5,6},{6,7},{7,8},{8,9},{9,10},{10,1... | collective-permute-start | bytes 1572872 | tf_op jit(solution)/shard_map/ppermute | solution.py:339
  19.9 56.2 %copy-start.1 = (bf16[512,512]{1,0:T(8,128)(2,1)S(1)}, bf16[512,512]{1,0:T(8,128)(2,1)}, u32[]{:S(2)}) copy-start(bf16[512,512]{1,0:T(8,128)(2,1)} %constant.18.clone.s_lo) | copy-start | bytes 1572868
  19.9 56.2 %copy-start.2 = (bf16[512,512]{1,0:T(8,128)(2,1)S(1)}, bf16[512,512]{1,0:T(8,128)(2,1)}, u32[]{:S(2)}) copy-start(bf16[512,512]{1,0:T(8,128)(2,1)} %constant.17.clone.s_hi) | copy-start | bytes 1572868
  19.9 56.1 %copy-start.3 = (f32[128,256]{1,0:T(8,128)S(1)}, f32[128,256]{1,0:T(8,128)}, u32[]{:S(2)}) copy-start(f32[128,256]{1,0:T(8,128)} %constant.20.clone.tw_s) | copy-start | bytes 393220
  20.0 56.1 %copy-start.4 = (f32[128,256]{1,0:T(8,128)S(1)}, f32[128,256]{1,0:T(8,128)}, u32[]{:S(2)}) copy-start(f32[128,256]{1,0:T(8,128)} %constant.19.clone.tw_c) | copy-start | bytes 393220
  20.0 56.1 %copy-start.5 = (bf16[256,256]{1,0:T(8,128)(2,1)S(1)}, bf16[256,256]{1,0:T(8,128)(2,1)}, u32[]{:S(2)}) copy-start(bf16[256,256]{1,0:T(8,128)(2,1)} %constant.16.clone.f_lo) | copy-start | bytes 393220
  20.0 56.1 %copy-start.6 = (bf16[256,256]{1,0:T(8,128)(2,1)S(1)}, bf16[256,256]{1,0:T(8,128)(2,1)}, u32[]{:S(2)}) copy-start(bf16[256,256]{1,0:T(8,128)(2,1)} %constant.15.clone.f_hi) | copy-start | bytes 393220
  20.0 56.1 %copy-start.8 = (s32[2,2]{1,0:T(2,128)S(1)}, s32[2,2]{1,0:T(2,128)}, u32[]{:S(2)}) copy-start(s32[2,2]{1,0:T(2,128)} %edges.1) | copy-start | bytes 52
  26.1 9.2 %collective-permute-start.4 = (f32[2,256,128]{2,1,0:T(8,128)S(1)}, f32[2,256,128]{2,1,0:T(8,128)S(1)}, u32[]{:S(2)}, u32[]{:S(2)}) collective-permute-start(f32[2,256,128]{2,1,0:T(8,128)S(1)} %get-tuple-element.17), channel_id=1, source_target_pairs={{0,192},{64,128},{128,64},{192,0},{1,193},{65,129},{129,65},{193,1... | collective-permute-start | bytes 786440 | tf_op jit(solution)/shard_map/ppermute | solution.py:331
  26.5 8.8 %collective-permute-start.1 = (f32[2,256,128]{2,1,0:T(8,128)S(1)}, f32[2,256,128]{2,1,0:T(8,128)S(1)}, u32[]{:S(2)}, u32[]{:S(2)}) collective-permute-start(f32[2,256,128]{2,1,0:T(8,128)S(1)} %get-tuple-element.18), channel_id=1, source_target_pairs={{0,64},{64,0},{128,192},{192,128},{1,65},{65,1},{129,193},{193,129... | collective-permute-start | bytes 786440 | tf_op jit(solution)/shard_map/ppermute | solution.py:331
  35.4 8.4 %collective-permute-start.3 = (f32[512,128]{1,0:T(8,128)S(1)}, f32[512,128]{1,0:T(8,128)S(1)}, u32[]{:S(2)}, u32[]{:S(2)}) collective-permute-start(f32[512,128]{1,0:T(8,128)S(1)} %pad_maximum_fusion), channel_id=1, source_target_pairs={{0,192},{64,128},{128,64},{192,0},{1,193},{65,129},{129,65},{193,1... | collective-permute-start | bytes 786440 | tf_op jit(solution)/shard_map/ppermute | solution.py:331
  36.7 7.1 %collective-permute-start.6 = (f32[512,128]{1,0:T(8,128)S(1)}, f32[512,128]{1,0:T(8,128)S(1)}, u32[]{:S(2)}, u32[]{:S(2)}) collective-permute-start(f32[512,128]{1,0:T(8,128)S(1)} %pad_maximum_fusion.1), channel_id=1, source_target_pairs={{0,64},{64,0},{128,192},{192,128},{1,65},{65,1},{129,193},{193,129... | collective-permute-start | bytes 786440 | tf_op jit(solution)/shard_map/ppermute | solution.py:331

commit v3 on v2

--- a/solution.py
+++ b/solution.py
@@ -22,10 +22,6 @@
     return lax.axis_index("aperture")
 
 
-def position(part, relative):
-    return (relative - 1) & 3 if part == 0 else 3 - relative
-
-
 def live(foot, slots, blocks):
     count = jnp.int32(0)
     for s in range(slots):
@@ -58,7 +54,7 @@
     start(1)
     own_copy.start()
     edge_copy.start()
-    for s in range(2, slots):
+    for s in range(2, 4):
         start(s)
     owns[blocks] = jnp.zeros((tall, depth), bf16)
     edges[blocks] = jnp.zeros((erows, depth), bf16)
@@ -92,6 +88,8 @@
     widen(1, wide1)
     own_copy.wait()
     edge_copy.wait()
+    for s in range(4, slots):
+        start(s)
 
     def step(s, here, there):
         arrive(s + 2)
@@ -110,9 +108,8 @@
     lax.fori_loop(0, (count + 3) // 4, quad, 0)
     for p in range(2):
         for j in range(4):
-            pos = position(p, me ^ j)
-            high_ref[p, pos] = sums[p, :tall, j * LANES:(j + 1) * LANES]
-            rim_ref[p, pos] = sums[p, tall:, j * LANES:(j + 1) * LANES]
+            high_ref[me ^ j, p] = sums[p, :tall, j * LANES:(j + 1) * LANES]
+            rim_ref[me ^ j, p] = sums[p, tall:, j * LANES:(j + 1) * LANES]
 
 
 def early_terms(sectors, foot, own, edge, begin):
@@ -126,7 +123,7 @@
         functools.partial(early_kernel, (slots, blocks, begin, tall, erows)),
         in_specs=[pl.BlockSpec(memory_space=pltpu.SMEM), hbm, hbm, hbm],
         out_specs=[vmem()] * 3,
-        out_shape=[jax.ShapeDtypeStruct((2, 4, r, quarter), f32) for r in (tall, erows)]
+        out_shape=[jax.ShapeDtypeStruct((4, 2, r, quarter), f32) for r in (tall, erows)]
         + [jax.ShapeDtypeStruct((slots, 2, depth, lines), bf16)],
         scratch_shapes=[
             pltpu.VMEM((2, tall + erows, lines), f32),
@@ -142,7 +139,7 @@
             flops=4 * slots * depth * lines * (tall + erows), bytes_accessed=slots * depth * lines * 4, transcendentals=0
         ),
         name="early_terms",
-    )(foot, *[pltpu.with_memory_space_constraint(v, pltpu.HBM) for v in (sectors, own, edge)])
+    )(pltpu.with_memory_space_constraint(foot, pltpu.HBM), *[pltpu.with_memory_space_constraint(v, pltpu.HBM) for v in (sectors, own, edge)])
 
 
 def late_kernel(cfg, foot, x_ref, own_ref, low_ref, sums):
@@ -166,7 +163,7 @@
         add(count - 1, (0,))
     for p in range(2):
         for j in range(4):
-            low_ref[p, position(p, me ^ j)] = sums[p, :, j * LANES:(j + 1) * LANES]
+            low_ref[me ^ j, p] = sums[p, :, j * LANES:(j + 1) * LANES]
 
 
 def late_terms(x, foot, own, tall):
@@ -176,38 +173,36 @@
         functools.partial(late_kernel, (slots, blocks, tall)),
         in_specs=[pl.BlockSpec(memory_space=pltpu.SMEM), vmem(), vmem()],
         out_specs=vmem(),
-        out_shape=jax.ShapeDtypeStruct((2, 4, tall, lines // 4), f32),
+        out_shape=jax.ShapeDtypeStruct((4, 2, tall, lines // 4), f32),
         scratch_shapes=[pltpu.VMEM((2, tall, lines), f32)],
         compiler_params=pltpu.CompilerParams(vmem_limit_bytes=24 << 20),
         cost_estimate=pl.CostEstimate(
             flops=4 * slots * depth * lines * tall, bytes_accessed=slots * depth * lines * 4, transcendentals=0
         ),
         name="late_terms",
-    )(foot, x, own)
-
-
-def pack_kernel(*refs):
+    )(pltpu.with_memory_space_constraint(foot, pltpu.HBM), x, own)
+
+
+def pack_kernel(lows, *refs):
     *terms, out_ref = refs
     for p in range(2):
-        keeps, firsts, second = terms[5 * p:5 * p + 2], terms[5 * p + 2:5 * p + 4], terms[5 * p + 4]
-        row = 0
-        for keep, first in zip(keeps, firsts):
-            for j in range(keep.shape[0] // LANES):
+        row = 4 * p
+        for group in (terms[:lows], terms[lows:]):
+            for j in range(group[0].shape[1] // LANES):
                 at = pl.ds(j * LANES, LANES)
-                total = keep[at] + first[at] + second[pl.ds(row * LANES, LANES)]
-                out_ref[pl.ds(4 * p + row, LANES, stride=8), :] = total.T
+                out_ref[pl.ds(row, LANES, stride=8), :] = sum(term[p, at] for term in group).T
                 row += 1
 
 
-def pack(*args):
+def pack(low, high):
     return pl.pallas_call(
-        pack_kernel,
-        in_specs=[vmem()] * len(args),
+        functools.partial(pack_kernel, len(low)),
+        in_specs=[vmem()] * (len(low) + len(high)),
         out_specs=vmem(),
         out_shape=jax.ShapeDtypeStruct((8 * LANES, LANES), f32),
         compiler_params=pltpu.CompilerParams(vmem_limit_bytes=8 << 20),
         name="pack",
-    )(*args)
+    )(*low, *high)
 
 
 def split(x):
@@ -337,13 +332,11 @@
     half = own_blocks.shape[1] // 2
     high, rim, spread = early_terms(sectors[0], foot, own_blocks, edge_blocks, half)
     incoming = lax.ppermute(rim, "tile", [(i, i + 1) for i in range(tiles - 1)])
-    ha, hb = swap(high[0, :2], 1), swap(high[1, :2], 3)
+    highs = [high[0]] + [swap(high[r], r) for r in (1, 3, 2)]
     low = late_terms(spread, foot, own_blocks, half)
     low = low + jnp.pad(incoming, ((0, 0), (0, 0), (0, half - incoming.shape[2]), (0, 0)))
-    la, lb = swap(low[0, :2], 1), swap(low[1, :2], 3)
-    qa = swap(jnp.concatenate([low[0, 2] + la[1], high[0, 2] + ha[1]]), 3)
-    qb = swap(jnp.concatenate([low[1, 2] + lb[1], high[1, 2] + hb[1]]), 1)
-    packed = pack(low[0, 3], high[0, 3], la[0], ha[0], qa, low[1, 3], high[1, 3], lb[0], hb[0], qb)
+    lows = [low[0]] + [swap(low[r], r) for r in (1, 3, 2)]
+    packed = pack(lows, highs)
     moved = lax.all_to_all(packed.reshape(tiles, 16, LANES), "tile", 0, 0, tiled=True)
     return image(edges, moved.reshape(tiles * 16, LANES), tiles * own_blocks.shape[1])
 

time: 78.3 us -> 74.7 us (0.954); the launches traced: 79.5 us -> 74.1 us
  Pallas kernels: 9.37 us -> 21 us
  starting transfers between devices: 18.5 us -> 10.4 us
  waiting for transfers between devices: 18.1 us -> 12.7 us
  blocking collectives: 32.1 us -> 29.7 us
  local copies, waits for them, and re-layouts: 1.03 us -> 0.19 us
    ppermute x6, starting transfers between devices: 16.6 us -> 8.44 us  [swap(): return lax.ppermute(block, 'aperture', [(i, i ^ flip) for i in range(4)])]
    pallas_call x1, Pallas kernels: 4.41 us -> 12.3 us  [early_terms(): pl.pallas_call(functools.partial(early_kernel, (slots, blocks, begin, tal...]
    ppermute x6, waiting for transfers between devices: 17.7 us -> 12.7 us  [swap(): return lax.ppermute(block, 'aperture', [(i, i ^ flip) for i in range(4)])]
    pallas_call x1, Pallas kernels: 1.42 us -> 5.22 us  [late_terms(): pl.pallas_call(functools.partial(late_kernel, (slots, blocks, tall)), in_...]
    all_to_all x1, blocking collectives: 32.1 us -> 29.7 us  [on_device(): lax.all_to_all(packed.reshape(tiles, 16, LANES), 'tile', 0, 0, tiled=True)]
    unnamed x18 -> x16, local copies, waits for them, and re-layouts: 0.88 us -> 0.04 us
  transfers between devices with their start and end apart: 7 -> 7, of which waited for: 5 -> 3; matrix products, arithmetic and copies ran while one was open for 0% -> 0% of each run, Pallas kernels for 2% -> 7%
where the time goes in v3:
time: 74.7 us; the launch traced here: 74.1 us
  blocking collectives  29.7 us (40%)
  Pallas kernels  21 us (28%)
  waiting for transfers between devices  12.7 us (17%)
  starting transfers between devices  10.4 us (14%)
    all_to_all x1, blocking collectives, on_device(): lax.all_to_all(packed.reshape(tiles, 16, LANES), 'tile', 0, 0, tiled=True)  29.7 us
    ppermute x6, waiting for transfers between devices, swap(): return lax.ppermute(block, 'aperture', [(i, i ^ flip) for i in range(4)])  12.7 us
    pallas_call x1, Pallas kernels, early_terms(): pl.pallas_call(functools.partial(early_kernel, (slots, blocks, begin, tal...  12.3 us
    ppermute x6, starting transfers between devices, swap(): return lax.ppermute(block, 'aperture', [(i, i ^ flip) for i in range(4)])  8.44 us
    pallas_call x1, Pallas kernels, late_terms(): pl.pallas_call(functools.partial(late_kernel, (slots, blocks, tall)), in_...  5.22 us
    pallas_call x1, Pallas kernels, image(): pl.pallas_call(image_kernel, in_specs=[pl.BlockSpec(memory_space=pltpu.SM...  3.25 us
    ppermute x1, starting transfers between devices, on_device(): incoming = lax.ppermute(rim, 'tile', [(i, i + 1) for i in range(tiles - 1)])  1.92 us
  transfers between devices with their start and end apart: 7, of which 3 were waited for; matrix products, arithmetic and copies ran while one was open for 0% of the time, Pallas kernels for 7%

profile of v3, /device:TPU:1, one launch (start us, length us, event | category | flops | bytes accessed | tf_op | source)
XLA Modules:
  0.0 74.1 jit_solution(17688350628405079143)
XLA Ops:
  0.0 12.3 %early_terms.1 = (f32[4,2,256,128]{3,2,1,0:T(8,128)S(1)}, f32[4,2,128,128]{3,2,1,0:T(8,128)S(1)}, bf16[12,2,512,512]{3,2,1,0:T(8,128)(2,1)S(1)}) custom-call(s32[2,12]{1,0:T(2,128)} %bitcast.33, bf16[12,4096,128]{2,1,0:T(8,128)(2,1)} %bitcast.35, bf16[6,512,512]{2,1,0:T(8,128)(2,1)} %own_ref.1, bf16[6,128,512]{2,1,0:T(8,128)(2,1)} %edge_hbm.1), custom_call_target="tpu_custom_call" | custom-call | flops 4831838208 | bytes 12582912 | tf_op jit(solution)/shard_map/early_terms/pallas_call | solution.py:122
  12.3 1.9 %collective-permute-start = (f32[4,2,128,128]{3,2,1,0:T(8,128)S(1)}, f32[4,2,128,128]{3,2,1,0:T(8,128)S(1)}, u32[]{:S(2)}, u32[]{:S(2)}) collective-permute-start(f32[4,2,128,128]{3,2,1,0:T(8,128)S(1)} %get-tuple-element.9), channel_id=1, source_target_pairs={{0,1},{1,2},{2,3},{3,4},{4,5},{5,6},{6,7},{7,8},{8,9},{9,10},{10,1... | collective-permute-start | bytes 1572872 | tf_op jit(solution)/shard_map/ppermute | solution.py:334
  14.3 0.1 slice_bitcast_fusion.4
  14.3 0.1 collective-permute-start.6
  14.4 4.4 %collective-permute-start.5 = (f32[2,256,128]{2,1,0:T(8,128)S(1)}, f32[2,256,128]{2,1,0:T(8,128)S(1)}, u32[]{:S(2)}, u32[]{:S(2)}) collective-permute-start(f32[2,256,128]{2,1,0:T(8,128)S(1)} %get-tuple-element.12), channel_id=1, source_target_pairs={{0,192},{64,128},{128,64},{192,0},{1,193},{65,129},{129,65},{193,1... | collective-permute-start | bytes 786440 | tf_op jit(solution)/shard_map/ppermute | solution.py:326
  18.9 0.0 collective-permute-start.4
  18.9 0.0 copy-start.3
  18.9 0.0 copy-start.4
  18.9 0.0 copy-start.5
  18.9 0.0 copy-start.6
  18.9 0.0 copy-start.7
  18.9 5.2 %late_terms.1 = f32[4,2,256,128]{3,2,1,0:T(8,128)S(1)} custom-call(s32[2,12]{1,0:T(2,128)} %bitcast.34, bf16[12,2,512,512]{3,2,1,0:T(8,128)(2,1)S(1)} %get-tuple-element.8.x_ref, bf16[6,512,512]{2,1,0:T(8,128)(2,1)S(1)} %copy-done), custom_call_target="tpu_custom_call" | custom-call | flops 3221225472 | bytes 12582912 | tf_op jit(solution)/shard_map/late_terms/pallas_call | solution.py:172
  24.2 0.0 collective-permute-done
  24.2 0.1 pad_add_fusion
  24.3 0.1 slice_bitcast_fusion
  24.4 0.1 collective-permute-start.3
  24.5 3.8 %collective-permute-start.2 = (f32[2,256,128]{2,1,0:T(8,128)S(1)}, f32[2,256,128]{2,1,0:T(8,128)S(1)}, u32[]{:S(2)}, u32[]{:S(2)}) collective-permute-start(f32[2,256,128]{2,1,0:T(8,128)S(1)} %get-tuple-element.16), channel_id=1, source_target_pairs={{0,192},{64,128},{128,64},{192,0},{1,193},{65,129},{129,65},{193,1... | collective-permute-start | bytes 786440 | tf_op jit(solution)/shard_map/ppermute | solution.py:326
  28.3 2.3 %collective-permute-done.5.refs_6_ = f32[2,256,128]{2,1,0:T(8,128)S(1)} collective-permute-done((f32[2,256,128]{2,1,0:T(8,128)S(1)}, f32[2,256,128]{2,1,0:T(8,128)S(1)}, u32[]{:S(2)}, u32[]{:S(2)}) %collective-permute-start.5) | collective-permute-done | bytes 262176 | tf_op jit(solution)/shard_map/ppermute | solution.py:326
  30.6 4.0 %collective-permute-done.3.refs_3_ = f32[2,256,128]{2,1,0:T(8,128)S(1)} collective-permute-done((f32[2,256,128]{2,1,0:T(8,128)S(1)}, f32[2,256,128]{2,1,0:T(8,128)S(1)}, u32[]{:S(2)}, u32[]{:S(2)}) %collective-permute-start.3) | collective-permute-done | bytes 262176 | tf_op jit(solution)/shard_map/ppermute | solution.py:326
  34.6 6.4 %collective-permute-done.2.refs_2_ = f32[2,256,128]{2,1,0:T(8,128)S(1)} collective-permute-done((f32[2,256,128]{2,1,0:T(8,128)S(1)}, f32[2,256,128]{2,1,0:T(8,128)S(1)}, u32[]{:S(2)}, u32[]{:S(2)}) %collective-permute-start.2) | collective-permute-done | bytes 262176 | tf_op jit(solution)/shard_map/ppermute | solution.py:326
  41.0 0.0 collective-permute-done.1.refs_1_
  41.0 0.2 pack.1
  41.2 29.7 %all_to_all.5 = f32[64,16,128]{2,1,0:T(8,128)S(1)} all-to-all(f32[64,16,128]{2,1,0:T(8,128)S(1)} %bitcast.31), channel_id=1, replica_groups=mesh['aperture'=4,'tile'=64] {'tile'}, dimensions={0} | all-to-all | bytes 1048576 | tf_op jit(solution)/shard_map/all_to_all | solution.py:340
  70.9 3.2 %image.1 = f32[2,512,128]{2,1,0:T(8,128)} custom-call(s32[2,2]{1,0:T(2,128)S(1)} %copy-done.7, f32[1024,128]{1,0:T(8,128)S(1)} %bitcast.32, bf16[256,256]{1,0:T(8,128)(2,1)S(1)} %copy-done.6, bf16[256,256]{1,0:T(8,128)(2,1)S(1)} %copy-done.5, bf16[512,512]{1,0:T(8,128)(2,1)S(1)} %copy-done.2, bf16[512,512]{1,0:T(8,128)(2,1)S(1)} %copy-done.1, ...), custom_call_target="tpu_custom_call" | custom-call | tf_op jit(solution)/shard_map/image/pallas_call | solution.py:313
  (14 shorter events, 0.0 us)
Async XLA Ops:
  0.0 18.9 %copy-start = (bf16[6,512,512]{2,1,0:T(8,128)(2,1)S(1)}, bf16[6,512,512]{2,1,0:T(8,128)(2,1)}, u32[]{:S(2)}) copy-start(bf16[6,512,512]{2,1,0:T(8,128)(2,1)} %own_ref.1) | copy-start | bytes 9437188
  12.3 11.8 %collective-permute-start = (f32[4,2,128,128]{3,2,1,0:T(8,128)S(1)}, f32[4,2,128,128]{3,2,1,0:T(8,128)S(1)}, u32[]{:S(2)}, u32[]{:S(2)}) collective-permute-start(f32[4,2,128,128]{3,2,1,0:T(8,128)S(1)} %get-tuple-element.9), channel_id=1, source_target_pairs={{0,1},{1,2},{2,3},{3,4},{4,5},{5,6},{6,7},{7,8},{8,9},{9,10},{10,1... | collective-permute-start | bytes 1572872 | tf_op jit(solution)/shard_map/ppermute | solution.py:334
  14.3 13.9 %collective-permute-start.6 = (f32[2,256,128]{2,1,0:T(8,128)S(1)}, f32[2,256,128]{2,1,0:T(8,128)S(1)}, u32[]{:S(2)}, u32[]{:S(2)}) collective-permute-start(f32[2,256,128]{2,1,0:T(8,128)S(1)} %get-tuple-element.11), channel_id=1, source_target_pairs={{0,128},{64,192},{128,0},{192,64},{1,129},{65,193},{129,1},{193,65... | collective-permute-start | bytes 786440 | tf_op jit(solution)/shard_map/ppermute | solution.py:326
  14.4 16.2 %collective-permute-start.5 = (f32[2,256,128]{2,1,0:T(8,128)S(1)}, f32[2,256,128]{2,1,0:T(8,128)S(1)}, u32[]{:S(2)}, u32[]{:S(2)}) collective-permute-start(f32[2,256,128]{2,1,0:T(8,128)S(1)} %get-tuple-element.12), channel_id=1, source_target_pairs={{0,192},{64,128},{128,64},{192,0},{1,193},{65,129},{129,65},{193,1... | collective-permute-start | bytes 786440 | tf_op jit(solution)/shard_map/ppermute | solution.py:326
  18.9 11.8 %collective-permute-start.4 = (f32[2,256,128]{2,1,0:T(8,128)S(1)}, f32[2,256,128]{2,1,0:T(8,128)S(1)}, u32[]{:S(2)}, u32[]{:S(2)}) collective-permute-start(f32[2,256,128]{2,1,0:T(8,128)S(1)} %get-tuple-element.13), channel_id=1, source_target_pairs={{0,64},{64,0},{128,192},{192,128},{1,65},{65,1},{129,193},{193,129... | collective-permute-start | bytes 786440 | tf_op jit(solution)/shard_map/ppermute | solution.py:326
  18.9 52.0 %copy-start.1 = (bf16[512,512]{1,0:T(8,128)(2,1)S(1)}, bf16[512,512]{1,0:T(8,128)(2,1)}, u32[]{:S(2)}) copy-start(bf16[512,512]{1,0:T(8,128)(2,1)} %constant.18.clone.s_lo) | copy-start | bytes 1572868
  18.9 52.0 %copy-start.2 = (bf16[512,512]{1,0:T(8,128)(2,1)S(1)}, bf16[512,512]{1,0:T(8,128)(2,1)}, u32[]{:S(2)}) copy-start(bf16[512,512]{1,0:T(8,128)(2,1)} %constant.17.clone.s_hi) | copy-start | bytes 1572868
  18.9 52.0 %copy-start.3 = (f32[128,256]{1,0:T(8,128)S(1)}, f32[128,256]{1,0:T(8,128)}, u32[]{:S(2)}) copy-start(f32[128,256]{1,0:T(8,128)} %constant.20.clone.tw_s) | copy-start | bytes 393220
  18.9 52.0 %copy-start.4 = (f32[128,256]{1,0:T(8,128)S(1)}, f32[128,256]{1,0:T(8,128)}, u32[]{:S(2)}) copy-start(f32[128,256]{1,0:T(8,128)} %constant.19.clone.tw_c) | copy-start | bytes 393220
  18.9 52.0 %copy-start.5 = (bf16[256,256]{1,0:T(8,128)(2,1)S(1)}, bf16[256,256]{1,0:T(8,128)(2,1)}, u32[]{:S(2)}) copy-start(bf16[256,256]{1,0:T(8,128)(2,1)} %constant.16.clone.f_lo) | copy-start | bytes 393220
  18.9 52.0 %copy-start.6 = (bf16[256,256]{1,0:T(8,128)(2,1)S(1)}, bf16[256,256]{1,0:T(8,128)(2,1)}, u32[]{:S(2)}) copy-start(bf16[256,256]{1,0:T(8,128)(2,1)} %constant.15.clone.f_hi) | copy-start | bytes 393220
  18.9 52.0 %copy-start.7 = (s32[2,2]{1,0:T(2,128)S(1)}, s32[2,2]{1,0:T(2,128)}, u32[]{:S(2)}) copy-start(s32[2,2]{1,0:T(2,128)} %edges.1) | copy-start | bytes 52
  24.4 10.2 %collective-permute-start.3 = (f32[2,256,128]{2,1,0:T(8,128)S(1)}, f32[2,256,128]{2,1,0:T(8,128)S(1)}, u32[]{:S(2)}, u32[]{:S(2)}) collective-permute-start(f32[2,256,128]{2,1,0:T(8,128)S(1)} %get-tuple-element.15), channel_id=1, source_target_pairs={{0,128},{64,192},{128,0},{192,64},{1,129},{65,193},{129,1},{193,65... | collective-permute-start | bytes 786440 | tf_op jit(solution)/shard_map/ppermute | solution.py:326
  24.5 16.5 %collective-permute-start.2 = (f32[2,256,128]{2,1,0:T(8,128)S(1)}, f32[2,256,128]{2,1,0:T(8,128)S(1)}, u32[]{:S(2)}, u32[]{:S(2)}) collective-permute-start(f32[2,256,128]{2,1,0:T(8,128)S(1)} %get-tuple-element.16), channel_id=1, source_target_pairs={{0,192},{64,128},{128,64},{192,0},{1,193},{65,129},{129,65},{193,1... | collective-permute-start | bytes 786440 | tf_op jit(solution)/shard_map/ppermute | solution.py:326
  28.3 12.7 %collective-permute-start.1 = (f32[2,256,128]{2,1,0:T(8,128)S(1)}, f32[2,256,128]{2,1,0:T(8,128)S(1)}, u32[]{:S(2)}, u32[]{:S(2)}) collective-permute-start(f32[2,256,128]{2,1,0:T(8,128)S(1)} %get-tuple-element.17), channel_id=1, source_target_pairs={{0,64},{64,0},{128,192},{192,128},{1,65},{65,1},{129,193},{193,129... | collective-permute-start | bytes 786440 | tf_op jit(solution)/shard_map/ppermute | solution.py:326

commit v4 on v3

--- a/solution.py
+++ b/solution.py
@@ -134,7 +134,7 @@
             pltpu.SemaphoreType.DMA((slots,)),
             pltpu.SemaphoreType.DMA((2,)),
         ],
-        compiler_params=pltpu.CompilerParams(vmem_limit_bytes=36 << 20),
+        compiler_params=pltpu.CompilerParams(vmem_limit_bytes=38 << 20),
         cost_estimate=pl.CostEstimate(
             flops=4 * slots * depth * lines * (tall + erows), bytes_accessed=slots * depth * lines * 4, transcendentals=0
         ),
@@ -329,14 +329,21 @@
 def on_device(sectors, footprint, own_blocks, edge_blocks, edges):
     tiles = lax.axis_size("tile")
     foot = footprint[0].T
-    half = own_blocks.shape[1] // 2
-    high, rim, spread = early_terms(sectors[0], foot, own_blocks, edge_blocks, half)
+    cut = edge_blocks.shape[1]
+    high, rim, spread = early_terms(sectors[0], foot, own_blocks, edge_blocks, cut)
     incoming = lax.ppermute(rim, "tile", [(i, i + 1) for i in range(tiles - 1)])
-    highs = [high[0]] + [swap(high[r], r) for r in (1, 3, 2)]
-    low = late_terms(spread, foot, own_blocks, half)
-    low = low + jnp.pad(incoming, ((0, 0), (0, 0), (0, half - incoming.shape[2]), (0, 0)))
-    lows = [low[0]] + [swap(low[r], r) for r in (1, 3, 2)]
-    packed = pack(lows, highs)
+    ha = swap(jnp.stack([high[1, 0], high[2, 0]]), 1)
+    hb = swap(jnp.stack([high[3, 1], high[2, 1]]), 3)
+    low = late_terms(spread, foot, own_blocks, cut) + incoming
+    la = swap(jnp.stack([low[1, 0], low[2, 0]]), 1)
+    lb = swap(jnp.stack([low[3, 1], low[2, 1]]), 3)
+    qa = swap(jnp.concatenate([low[3, 0] + la[1], high[3, 0] + ha[1]]), 3)
+    qb = swap(jnp.concatenate([low[1, 1] + lb[1], high[1, 1] + hb[1]]), 1)
+    q = jnp.stack([qa, qb])
+    packed = pack(
+        [low[0], jnp.stack([la[0], lb[0]]), q[:, :cut]],
+        [high[0], jnp.stack([ha[0], hb[0]]), q[:, cut:]],
+    )
     moved = lax.all_to_all(packed.reshape(tiles, 16, LANES), "tile", 0, 0, tiled=True)
     return image(edges, moved.reshape(tiles * 16, LANES), tiles * own_blocks.shape[1])
 

time: 74.7 us -> 76.5 us (1.024); the launches traced: 74.1 us -> 76.8 us
  Pallas kernels: 21 us -> 9.73 us
  blocking collectives: 29.7 us -> 38.3 us
  waiting for transfers between devices: 12.7 us -> 16.5 us
  starting transfers between devices: 10.4 us -> 11.5 us
    all_to_all x1, blocking collectives: 29.7 us -> 38.3 us  [on_device(): lax.all_to_all(packed.reshape(tiles, 16, LANES), 'tile', 0, 0, tiled=True)]
    pallas_call x1, Pallas kernels: 12.3 us -> 5.03 us  [early_terms(): pl.pallas_call(functools.partial(early_kernel, (slots, blocks, begin, tal...]
    pallas_call x1, Pallas kernels: 5.22 us -> 1.2 us  [late_terms(): pl.pallas_call(functools.partial(late_kernel, (slots, blocks, tall)), in_...]
    ppermute x1, starting transfers between devices: 1.92 us -> 4.61 us  [on_device(): incoming = lax.ppermute(rim, 'tile', [(i, i + 1) for i in range(tiles - 1)])]
    ppermute x6, waiting for transfers between devices: 12.7 us -> 14.7 us  [swap(): return lax.ppermute(block, 'aperture', [(i, i ^ flip) for i in range(4)])]
    ppermute x1, waiting for transfers between devices: 0.01 us -> 1.8 us  [on_device(): incoming = lax.ppermute(rim, 'tile', [(i, i + 1) for i in range(tiles - 1)])]
    ppermute x6, starting transfers between devices: 8.44 us -> 6.85 us  [swap(): return lax.ppermute(block, 'aperture', [(i, i ^ flip) for i in range(4)])]
  transfers between devices with their start and end apart: 7 -> 7, of which waited for: 3 -> 7; matrix products, arithmetic and copies ran while one was open for 0% -> 1% of each run, Pallas kernels for 7% -> 2%
where the time goes in v4:
time: 76.5 us; the launch traced here: 76.8 us
  blocking collectives  38.3 us (50%)
  waiting for transfers between devices  16.5 us (22%)
  starting transfers between devices  11.5 us (15%)
  Pallas kernels  9.73 us (13%)
    all_to_all x1, blocking collectives, on_device(): lax.all_to_all(packed.reshape(tiles, 16, LANES), 'tile', 0, 0, tiled=True)  38.3 us
    ppermute x6, waiting for transfers between devices, swap(): return lax.ppermute(block, 'aperture', [(i, i ^ flip) for i in range(4)])  14.7 us
    ppermute x6, starting transfers between devices, swap(): return lax.ppermute(block, 'aperture', [(i, i ^ flip) for i in range(4)])  6.85 us
    pallas_call x1, Pallas kernels, early_terms(): pl.pallas_call(functools.partial(early_kernel, (slots, blocks, begin, tal...  5.03 us
    ppermute x1, starting transfers between devices, on_device(): incoming = lax.ppermute(rim, 'tile', [(i, i + 1) for i in range(tiles - 1)])  4.61 us
    pallas_call x1, Pallas kernels, image(): pl.pallas_call(image_kernel, in_specs=[pl.BlockSpec(memory_space=pltpu.SM...  3.26 us
    ppermute x1, waiting for transfers between devices, on_device(): incoming = lax.ppermute(rim, 'tile', [(i, i + 1) for i in range(tiles - 1)])  1.8 us
  transfers between devices with their start and end apart: 7, of which 7 were waited for; matrix products, arithmetic and copies ran while one was open for 1% of the time, Pallas kernels for 2%

profile of v4, /device:TPU:1, one launch (start us, length us, event | category | flops | bytes accessed | tf_op | source)
XLA Modules:
  0.0 76.8 jit_solution(18156522648217161450)
XLA Ops:
  0.0 5.0 %early_terms.1 = (f32[4,2,384,128]{3,2,1,0:T(8,128)S(1)}, f32[4,2,128,128]{3,2,1,0:T(8,128)S(1)}, bf16[12,2,512,512]{3,2,1,0:T(8,128)(2,1)S(1)}) custom-call(s32[2,12]{1,0:T(2,128)} %bitcast.71, bf16[12,4096,128]{2,1,0:T(8,128)(2,1)} %bitcast.73, bf16[6,512,512]{2,1,0:T(8,128)(2,1)} %own_ref.1, bf16[6,128,512]{2,1,0:T(8,128)(2,1)} %edge_hbm.1), custom_call_target="tpu_custom_call" | custom-call | flops 6442450944 | bytes 12582912 | tf_op jit(solution)/shard_map/early_terms/pallas_call | solution.py:122
  5.0 4.6 %collective-permute-start = (f32[4,2,128,128]{3,2,1,0:T(8,128)S(1)}, f32[4,2,128,128]{3,2,1,0:T(8,128)S(1)}, u32[]{:S(2)}, u32[]{:S(2)}) collective-permute-start(f32[4,2,128,128]{3,2,1,0:T(8,128)S(1)} %get-tuple-element.9), channel_id=1, source_target_pairs={{0,1},{1,2},{2,3},{3,4},{4,5},{5,6},{6,7},{7,8},{8,9},{9,10},{10,1... | collective-permute-start | bytes 1572872 | tf_op jit(solution)/shard_map/ppermute | solution.py:334
  9.7 0.1 slice_bitcast_fusion.6
  9.8 2.6 %collective-permute-start.5 = (f32[2,384,128]{2,1,0:T(8,128)S(1)}, f32[2,384,128]{2,1,0:T(8,128)S(1)}, u32[]{:S(2)}, u32[]{:S(2)}) collective-permute-start(f32[2,384,128]{2,1,0:T(8,128)S(1)} %pad_maximum_fusion.2), channel_id=1, source_target_pairs={{0,192},{64,128},{128,64},{192,0},{1,193},{65,129},{129,65},{193,1... | collective-permute-start | bytes 1179656 | tf_op jit(solution)/shard_map/ppermute | solution.py:326
  12.4 0.3 collective-permute-start.3
  12.7 1.2 %late_terms.1 = f32[4,2,128,128]{3,2,1,0:T(8,128)S(1)} custom-call(s32[2,12]{1,0:T(2,128)} %bitcast.72, bf16[12,2,512,512]{3,2,1,0:T(8,128)(2,1)S(1)} %get-tuple-element.8.x_ref, bf16[6,512,512]{2,1,0:T(8,128)(2,1)S(1)} %copy-done), custom_call_target="tpu_custom_call" | custom-call | flops 1610612736 | bytes 12582912 | tf_op jit(solution)/shard_map/late_terms/pallas_call | solution.py:172
  14.0 1.8 %collective-permute-done = f32[4,2,128,128]{3,2,1,0:T(8,128)S(1)} collective-permute-done((f32[4,2,128,128]{3,2,1,0:T(8,128)S(1)}, f32[4,2,128,128]{3,2,1,0:T(8,128)S(1)}, u32[]{:S(2)}, u32[]{:S(2)}) %collective-permute-start) | collective-permute-done | bytes 524320 | tf_op jit(solution)/shard_map/ppermute | solution.py:334
  15.8 0.1 add.15
  15.9 2.6 %collective-permute-start.2 = (f32[2,128,128]{2,1,0:T(8,128)S(1)}, f32[2,128,128]{2,1,0:T(8,128)S(1)}, u32[]{:S(2)}, u32[]{:S(2)}) collective-permute-start(f32[2,128,128]{2,1,0:T(8,128)S(1)} %pad_maximum_fusion.8), channel_id=1, source_target_pairs={{0,192},{64,128},{128,64},{192,0},{1,193},{65,129},{129,65},{193,1... | collective-permute-start | bytes 393224 | tf_op jit(solution)/shard_map/ppermute | solution.py:326
  18.4 0.3 collective-permute-start.1
  18.8 3.3 %collective-permute-done.5 = f32[2,384,128]{2,1,0:T(8,128)S(1)} collective-permute-done((f32[2,384,128]{2,1,0:T(8,128)S(1)}, f32[2,384,128]{2,1,0:T(8,128)S(1)}, u32[]{:S(2)}, u32[]{:S(2)}) %collective-permute-start.5) | collective-permute-done | bytes 393248 | tf_op jit(solution)/shard_map/ppermute | solution.py:326
  22.1 1.4 %collective-permute-done.3 = f32[2,384,128]{2,1,0:T(8,128)S(1)} collective-permute-done((f32[2,384,128]{2,1,0:T(8,128)S(1)}, f32[2,384,128]{2,1,0:T(8,128)S(1)}, u32[]{:S(2)}, u32[]{:S(2)}) %collective-permute-start.3) | collective-permute-done | bytes 393248 | tf_op jit(solution)/shard_map/ppermute | solution.py:326
  23.7 1.2 %collective-permute-done.2 = f32[2,128,128]{2,1,0:T(8,128)S(1)} collective-permute-done((f32[2,128,128]{2,1,0:T(8,128)S(1)}, f32[2,128,128]{2,1,0:T(8,128)S(1)}, u32[]{:S(2)}, u32[]{:S(2)}) %collective-permute-start.2) | collective-permute-done | bytes 131104 | tf_op jit(solution)/shard_map/ppermute | solution.py:326
  24.9 0.5 collective-permute-done.1
  25.5 0.1 collective-permute-start.6
  25.7 0.9 %collective-permute-start.4 = (f32[512,128]{1,0:T(8,128)S(1)}, f32[512,128]{1,0:T(8,128)S(1)}, u32[]{:S(2)}, u32[]{:S(2)}) collective-permute-start(f32[512,128]{1,0:T(8,128)S(1)} %pad_maximum_fusion.4), channel_id=1, source_target_pairs={{0,192},{64,128},{128,64},{192,0},{1,193},{65,129},{129,65},{193,1... | collective-permute-start | bytes 786440 | tf_op jit(solution)/shard_map/ppermute | solution.py:326
  26.7 6.7 %collective-permute-done.6 = f32[512,128]{1,0:T(8,128)S(1)} collective-permute-done((f32[512,128]{1,0:T(8,128)S(1)}, f32[512,128]{1,0:T(8,128)S(1)}, u32[]{:S(2)}, u32[]{:S(2)}) %collective-permute-start.6) | collective-permute-done | bytes 262176 | tf_op jit(solution)/shard_map/ppermute | solution.py:326
  33.4 1.3 %collective-permute-done.4 = f32[512,128]{1,0:T(8,128)S(1)} collective-permute-done((f32[512,128]{1,0:T(8,128)S(1)}, f32[512,128]{1,0:T(8,128)S(1)}, u32[]{:S(2)}, u32[]{:S(2)}) %collective-permute-start.4) | collective-permute-done | bytes 262176 | tf_op jit(solution)/shard_map/ppermute | solution.py:326
  34.8 0.0 copy-start.2
  34.8 0.0 copy-start.3
  34.8 0.0 copy-start.4
  34.9 0.2 pack.1
  35.1 38.3 %all_to_all.5 = f32[64,16,128]{2,1,0:T(8,128)S(1)} all-to-all(f32[64,16,128]{2,1,0:T(8,128)S(1)} %bitcast.66), channel_id=1, replica_groups=mesh['aperture'=4,'tile'=64] {'tile'}, dimensions={0} | all-to-all | bytes 1048576 | tf_op jit(solution)/shard_map/all_to_all | solution.py:347
  73.5 3.3 %image.1 = f32[2,512,128]{2,1,0:T(8,128)} custom-call(s32[2,2]{1,0:T(2,128)S(1)} %copy-done.7, f32[1024,128]{1,0:T(8,128)S(1)} %bitcast.65, bf16[256,256]{1,0:T(8,128)(2,1)S(1)} %copy-done.6, bf16[256,256]{1,0:T(8,128)(2,1)S(1)} %copy-done.5, bf16[512,512]{1,0:T(8,128)(2,1)S(1)} %copy-done.2, bf16[512,512]{1,0:T(8,128)(2,1)S(1)} %copy-done.1, ...), custom_call_target="tpu_custom_call" | custom-call | tf_op jit(solution)/shard_map/image/pallas_call | solution.py:313
  (32 shorter events, 0.4 us)
Async XLA Ops:
  5.0 10.7 %collective-permute-start = (f32[4,2,128,128]{3,2,1,0:T(8,128)S(1)}, f32[4,2,128,128]{3,2,1,0:T(8,128)S(1)}, u32[]{:S(2)}, u32[]{:S(2)}) collective-permute-start(f32[4,2,128,128]{3,2,1,0:T(8,128)S(1)} %get-tuple-element.9), channel_id=1, source_target_pairs={{0,1},{1,2},{2,3},{3,4},{4,5},{5,6},{6,7},{7,8},{8,9},{9,10},{10,1... | collective-permute-start | bytes 1572872 | tf_op jit(solution)/shard_map/ppermute | solution.py:334
  9.6 3.1 %copy-start = (bf16[6,512,512]{2,1,0:T(8,128)(2,1)S(1)}, bf16[6,512,512]{2,1,0:T(8,128)(2,1)}, u32[]{:S(2)}) copy-start(bf16[6,512,512]{2,1,0:T(8,128)(2,1)} %own_ref.1) | copy-start | bytes 9437188
  9.8 12.4 %collective-permute-start.5 = (f32[2,384,128]{2,1,0:T(8,128)S(1)}, f32[2,384,128]{2,1,0:T(8,128)S(1)}, u32[]{:S(2)}, u32[]{:S(2)}) collective-permute-start(f32[2,384,128]{2,1,0:T(8,128)S(1)} %pad_maximum_fusion.2), channel_id=1, source_target_pairs={{0,192},{64,128},{128,64},{192,0},{1,193},{65,129},{129,65},{193,1... | collective-permute-start | bytes 1179656 | tf_op jit(solution)/shard_map/ppermute | solution.py:326
  12.4 11.2 %collective-permute-start.3 = (f32[2,384,128]{2,1,0:T(8,128)S(1)}, f32[2,384,128]{2,1,0:T(8,128)S(1)}, u32[]{:S(2)}, u32[]{:S(2)}) collective-permute-start(f32[2,384,128]{2,1,0:T(8,128)S(1)} %pad_maximum_fusion.1), channel_id=1, source_target_pairs={{0,64},{64,0},{128,192},{192,128},{1,65},{65,1},{129,193},{193,129... | collective-permute-start | bytes 1179656 | tf_op jit(solution)/shard_map/ppermute | solution.py:326
  15.9 9.1 %collective-permute-start.2 = (f32[2,128,128]{2,1,0:T(8,128)S(1)}, f32[2,128,128]{2,1,0:T(8,128)S(1)}, u32[]{:S(2)}, u32[]{:S(2)}) collective-permute-start(f32[2,128,128]{2,1,0:T(8,128)S(1)} %pad_maximum_fusion.8), channel_id=1, source_target_pairs={{0,192},{64,128},{128,64},{192,0},{1,193},{65,129},{129,65},{193,1... | collective-permute-start | bytes 393224 | tf_op jit(solution)/shard_map/ppermute | solution.py:326
  18.4 7.0 %collective-permute-start.1 = (f32[2,128,128]{2,1,0:T(8,128)S(1)}, f32[2,128,128]{2,1,0:T(8,128)S(1)}, u32[]{:S(2)}, u32[]{:S(2)}) collective-permute-start(f32[2,128,128]{2,1,0:T(8,128)S(1)} %pad_maximum_fusion.7), channel_id=1, source_target_pairs={{0,64},{64,0},{128,192},{192,128},{1,65},{65,1},{129,193},{193,129... | collective-permute-start | bytes 393224 | tf_op jit(solution)/shard_map/ppermute | solution.py:326
  25.5 7.9 %collective-permute-start.6 = (f32[512,128]{1,0:T(8,128)S(1)}, f32[512,128]{1,0:T(8,128)S(1)}, u32[]{:S(2)}, u32[]{:S(2)}) collective-permute-start(f32[512,128]{1,0:T(8,128)S(1)} %pad_maximum_fusion.5), channel_id=1, source_target_pairs={{0,64},{64,0},{128,192},{192,128},{1,65},{65,1},{129,193},{193,129... | collective-permute-start | bytes 786440 | tf_op jit(solution)/shard_map/ppermute | solution.py:326
  25.7 9.1 %collective-permute-start.4 = (f32[512,128]{1,0:T(8,128)S(1)}, f32[512,128]{1,0:T(8,128)S(1)}, u32[]{:S(2)}, u32[]{:S(2)}) collective-permute-start(f32[512,128]{1,0:T(8,128)S(1)} %pad_maximum_fusion.4), channel_id=1, source_target_pairs={{0,192},{64,128},{128,64},{192,0},{1,193},{65,129},{129,65},{193,1... | collective-permute-start | bytes 786440 | tf_op jit(solution)/shard_map/ppermute | solution.py:326
  34.8 38.7 %copy-start.1 = (bf16[512,512]{1,0:T(8,128)(2,1)S(1)}, bf16[512,512]{1,0:T(8,128)(2,1)}, u32[]{:S(2)}) copy-start(bf16[512,512]{1,0:T(8,128)(2,1)} %constant.15.clone.s_lo) | copy-start | bytes 1572868
  34.8 38.7 %copy-start.2 = (bf16[512,512]{1,0:T(8,128)(2,1)S(1)}, bf16[512,512]{1,0:T(8,128)(2,1)}, u32[]{:S(2)}) copy-start(bf16[512,512]{1,0:T(8,128)(2,1)} %constant.14.clone.s_hi) | copy-start | bytes 1572868
  34.8 38.6 %copy-start.3 = (f32[128,256]{1,0:T(8,128)S(1)}, f32[128,256]{1,0:T(8,128)}, u32[]{:S(2)}) copy-start(f32[128,256]{1,0:T(8,128)} %constant.17.clone.tw_s) | copy-start | bytes 393220
  34.8 38.6 %copy-start.4 = (f32[128,256]{1,0:T(8,128)S(1)}, f32[128,256]{1,0:T(8,128)}, u32[]{:S(2)}) copy-start(f32[128,256]{1,0:T(8,128)} %constant.16.clone.tw_c) | copy-start | bytes 393220
  34.8 38.6 %copy-start.5 = (bf16[256,256]{1,0:T(8,128)(2,1)S(1)}, bf16[256,256]{1,0:T(8,128)(2,1)}, u32[]{:S(2)}) copy-start(bf16[256,256]{1,0:T(8,128)(2,1)} %constant.13.clone.f_lo) | copy-start | bytes 393220
  34.9 38.6 %copy-start.6 = (bf16[256,256]{1,0:T(8,128)(2,1)S(1)}, bf16[256,256]{1,0:T(8,128)(2,1)}, u32[]{:S(2)}) copy-start(bf16[256,256]{1,0:T(8,128)(2,1)} %constant.12.clone.f_hi) | copy-start | bytes 393220
  34.9 38.6 %copy-start.7 = (s32[2,2]{1,0:T(2,128)S(1)}, s32[2,2]{1,0:T(2,128)}, u32[]{:S(2)}) copy-start(s32[2,2]{1,0:T(2,128)} %edges.1) | copy-start | bytes 52

commit v5 on v4

--- a/solution.py
+++ b/solution.py
@@ -335,14 +335,10 @@
     ha = swap(jnp.stack([high[1, 0], high[2, 0]]), 1)
     hb = swap(jnp.stack([high[3, 1], high[2, 1]]), 3)
     low = late_terms(spread, foot, own_blocks, cut) + incoming
-    la = swap(jnp.stack([low[1, 0], low[2, 0]]), 1)
-    lb = swap(jnp.stack([low[3, 1], low[2, 1]]), 3)
-    qa = swap(jnp.concatenate([low[3, 0] + la[1], high[3, 0] + ha[1]]), 3)
-    qb = swap(jnp.concatenate([low[1, 1] + lb[1], high[1, 1] + hb[1]]), 1)
-    q = jnp.stack([qa, qb])
+    qa, qb = swap(high[3, 0] + ha[1], 3), swap(high[1, 1] + hb[1], 1)
     packed = pack(
-        [low[0], jnp.stack([la[0], lb[0]]), q[:, :cut]],
-        [high[0], jnp.stack([ha[0], hb[0]]), q[:, cut:]],
+        [low[0]] + [swap(low[r], r) for r in (1, 3, 2)],
+        [high[0], jnp.stack([ha[0], hb[0]]), jnp.stack([qa, qb])],
     )
     moved = lax.all_to_all(packed.reshape(tiles, 16, LANES), "tile", 0, 0, tiled=True)
     return image(edges, moved.reshape(tiles * 16, LANES), tiles * own_blocks.shape[1])

time: 76.5 us -> 77.2 us (level); the launches traced: 76.8 us -> 75.7 us
  starting transfers between devices: 11.5 us -> 20.5 us
  blocking collectives: 38.3 us -> 33.2 us
  waiting for transfers between devices: 16.5 us -> 12 us
    ppermute x6 -> x7, starting transfers between devices: 6.85 us -> 15.3 us  [swap(): return lax.ppermute(block, 'aperture', [(i, i ^ flip) for i in range(4)])]
    all_to_all x1, blocking collectives: 38.3 us -> 33.2 us  [on_device(): lax.all_to_all(packed.reshape(tiles, 16, LANES), 'tile', 0, 0, tiled=True)]
    ppermute x6 -> x7, waiting for transfers between devices: 14.7 us -> 12 us  [swap(): return lax.ppermute(block, 'aperture', [(i, i ^ flip) for i in range(4)])]
    ppermute x1, waiting for transfers between devices: 1.8 us -> 0.01 us  [on_device(): incoming = lax.ppermute(rim, 'tile', [(i, i + 1) for i in range(tiles - 1)])]
  transfers between devices with their start and end apart: 7 -> 8, of which waited for: 7 -> 5; matrix products, arithmetic and copies ran while one was open for 1% -> 0% of each run, Pallas kernels for 2% -> 1%
where the time goes in v5:
time: 77.2 us; the launch traced here: 75.7 us
  blocking collectives  33.2 us (43%)
  starting transfers between devices  20.5 us (27%)
  waiting for transfers between devices  12 us (16%)
  Pallas kernels  9.35 us (12%)
    all_to_all x1, blocking collectives, on_device(): lax.all_to_all(packed.reshape(tiles, 16, LANES), 'tile', 0, 0, tiled=True)  33.2 us
    ppermute x7, starting transfers between devices, swap(): return lax.ppermute(block, 'aperture', [(i, i ^ flip) for i in range(4)])  15.3 us
    ppermute x7, waiting for transfers between devices, swap(): return lax.ppermute(block, 'aperture', [(i, i ^ flip) for i in range(4)])  12 us
    ppermute x1, starting transfers between devices, on_device(): incoming = lax.ppermute(rim, 'tile', [(i, i + 1) for i in range(tiles - 1)])  5.24 us
    pallas_call x1, Pallas kernels, early_terms(): pl.pallas_call(functools.partial(early_kernel, (slots, blocks, begin, tal...  4.71 us
    pallas_call x1, Pallas kernels, image(): pl.pallas_call(image_kernel, in_specs=[pl.BlockSpec(memory_space=pltpu.SM...  3.35 us
  transfers between devices with their start and end apart: 8, of which 5 were waited for; matrix products, arithmetic and copies ran while one was open for 0% of the time, Pallas kernels for 1%

profile of v5, /device:TPU:1, one launch (start us, length us, event | category | flops | bytes accessed | tf_op | source)
XLA Modules:
  0.0 75.7 jit_solution(7764082096544570465)
XLA Ops:
  0.0 4.7 %early_terms.1 = (f32[4,2,384,128]{3,2,1,0:T(8,128)S(1)}, f32[4,2,128,128]{3,2,1,0:T(8,128)S(1)}, bf16[12,2,512,512]{3,2,1,0:T(8,128)(2,1)S(1)}) custom-call(s32[2,12]{1,0:T(2,128)} %bitcast.51, bf16[12,4096,128]{2,1,0:T(8,128)(2,1)} %bitcast.53, bf16[6,512,512]{2,1,0:T(8,128)(2,1)} %own_ref.1, bf16[6,128,512]{2,1,0:T(8,128)(2,1)} %edge_hbm.1), custom_call_target="tpu_custom_call" | custom-call | flops 6442450944 | bytes 12582912 | tf_op jit(solution)/shard_map/early_terms/pallas_call | solution.py:122
  4.7 5.2 %collective-permute-start = (f32[4,2,128,128]{3,2,1,0:T(8,128)S(1)}, f32[4,2,128,128]{3,2,1,0:T(8,128)S(1)}, u32[]{:S(2)}, u32[]{:S(2)}) collective-permute-start(f32[4,2,128,128]{3,2,1,0:T(8,128)S(1)} %get-tuple-element.9), channel_id=1, source_target_pairs={{0,1},{1,2},{2,3},{3,4},{4,5},{5,6},{6,7},{7,8},{8,9},{9,10},{10,1... | collective-permute-start | bytes 1572872 | tf_op jit(solution)/shard_map/ppermute | solution.py:334
  10.0 0.0 copy-start
  10.0 0.1 slice_bitcast_fusion.6
  10.1 2.6 %collective-permute-start.5 = (f32[2,384,128]{2,1,0:T(8,128)S(1)}, f32[2,384,128]{2,1,0:T(8,128)S(1)}, u32[]{:S(2)}, u32[]{:S(2)}) collective-permute-start(f32[2,384,128]{2,1,0:T(8,128)S(1)} %pad_maximum_fusion.1), channel_id=1, source_target_pairs={{0,192},{64,128},{128,64},{192,0},{1,193},{65,129},{129,65},{193,1... | collective-permute-start | bytes 1179656 | tf_op jit(solution)/shard_map/ppermute | solution.py:326
  12.7 5.3 %collective-permute-start.4 = (f32[2,384,128]{2,1,0:T(8,128)S(1)}, f32[2,384,128]{2,1,0:T(8,128)S(1)}, u32[]{:S(2)}, u32[]{:S(2)}) collective-permute-start(f32[2,384,128]{2,1,0:T(8,128)S(1)} %pad_maximum_fusion), channel_id=1, source_target_pairs={{0,64},{64,0},{128,192},{192,128},{1,65},{65,1},{129,193},{193,129... | collective-permute-start | bytes 1179656 | tf_op jit(solution)/shard_map/ppermute | solution.py:326
  18.0 1.1 %late_terms.1 = f32[4,2,128,128]{3,2,1,0:T(8,128)S(1)} custom-call(s32[2,12]{1,0:T(2,128)} %bitcast.52, bf16[12,2,512,512]{3,2,1,0:T(8,128)(2,1)S(1)} %get-tuple-element.8.x_ref, bf16[6,512,512]{2,1,0:T(8,128)(2,1)S(1)} %copy-done), custom_call_target="tpu_custom_call" | custom-call | flops 1610612736 | bytes 12582912 | tf_op jit(solution)/shard_map/late_terms/pallas_call | solution.py:172
  19.1 6.0 %collective-permute-done.4 = f32[2,384,128]{2,1,0:T(8,128)S(1)} collective-permute-done((f32[2,384,128]{2,1,0:T(8,128)S(1)}, f32[2,384,128]{2,1,0:T(8,128)S(1)}, u32[]{:S(2)}, u32[]{:S(2)}) %collective-permute-start.4) | collective-permute-done | bytes 393248 | tf_op jit(solution)/shard_map/ppermute | solution.py:326
  25.2 3.5 %collective-permute-start.6 = (f32[384,128]{1,0:T(8,128)S(1)}, f32[384,128]{1,0:T(8,128)S(1)}, u32[]{:S(2)}, u32[]{:S(2)}) collective-permute-start(f32[384,128]{1,0:T(8,128)S(1)} %get-tuple-element.11), channel_id=1, source_target_pairs={{0,192},{64,128},{128,64},{192,0},{1,193},{65,129},{129,65},{193,1... | collective-permute-start | bytes 589832 | tf_op jit(solution)/shard_map/ppermute | solution.py:326
  28.6 0.8 %collective-permute-start.7 = (f32[384,128]{1,0:T(8,128)S(1)}, f32[384,128]{1,0:T(8,128)S(1)}, u32[]{:S(2)}, u32[]{:S(2)}) collective-permute-start(f32[384,128]{1,0:T(8,128)S(1)} %get-tuple-element.12), channel_id=1, source_target_pairs={{0,64},{64,0},{128,192},{192,128},{1,65},{65,1},{129,193},{193,129... | collective-permute-start | bytes 589832 | tf_op jit(solution)/shard_map/ppermute | solution.py:326
  29.5 0.0 collective-permute-done
  29.5 0.1 add.9
  29.6 0.6 collective-permute-start.3
  30.2 2.6 %collective-permute-start.2 = (f32[2,128,128]{2,1,0:T(8,128)S(1)}, f32[2,128,128]{2,1,0:T(8,128)S(1)}, u32[]{:S(2)}, u32[]{:S(2)}) collective-permute-start(f32[2,128,128]{2,1,0:T(8,128)S(1)} %get-tuple-element.18), channel_id=1, source_target_pairs={{0,192},{64,128},{128,64},{192,0},{1,193},{65,129},{129,65},{193,1... | collective-permute-start | bytes 393224 | tf_op jit(solution)/shard_map/ppermute | solution.py:326
  32.8 0.7 collective-permute-done.7
  33.5 2.8 %collective-permute-done.3.refs_3_ = f32[2,128,128]{2,1,0:T(8,128)S(1)} collective-permute-done((f32[2,128,128]{2,1,0:T(8,128)S(1)}, f32[2,128,128]{2,1,0:T(8,128)S(1)}, u32[]{:S(2)}, u32[]{:S(2)}) %collective-permute-start.3) | collective-permute-done | bytes 131104 | tf_op jit(solution)/shard_map/ppermute | solution.py:326
  36.3 0.9 %collective-permute-done.2.refs_2_ = f32[2,128,128]{2,1,0:T(8,128)S(1)} collective-permute-done((f32[2,128,128]{2,1,0:T(8,128)S(1)}, f32[2,128,128]{2,1,0:T(8,128)S(1)}, u32[]{:S(2)}, u32[]{:S(2)}) %collective-permute-start.2) | collective-permute-done | bytes 131104 | tf_op jit(solution)/shard_map/ppermute | solution.py:326
  37.2 1.6 %collective-permute-done.1.refs_1_ = f32[2,128,128]{2,1,0:T(8,128)S(1)} collective-permute-done((f32[2,128,128]{2,1,0:T(8,128)S(1)}, f32[2,128,128]{2,1,0:T(8,128)S(1)}, u32[]{:S(2)}, u32[]{:S(2)}) %collective-permute-start.1) | collective-permute-done | bytes 131104 | tf_op jit(solution)/shard_map/ppermute | solution.py:326
  38.8 0.0 copy-start.5
  38.8 0.0 copy-start.6
  38.8 0.0 copy-start.7
  38.9 0.2 pack.1
  39.1 33.2 %all_to_all.5 = f32[64,16,128]{2,1,0:T(8,128)S(1)} all-to-all(f32[64,16,128]{2,1,0:T(8,128)S(1)} %bitcast.47), channel_id=1, replica_groups=mesh['aperture'=4,'tile'=64] {'tile'}, dimensions={0} | all-to-all | bytes 1048576 | tf_op jit(solution)/shard_map/all_to_all | solution.py:343
  72.3 3.3 %image.1 = f32[2,512,128]{2,1,0:T(8,128)} custom-call(s32[2,2]{1,0:T(2,128)S(1)} %copy-done.7, f32[1024,128]{1,0:T(8,128)S(1)} %bitcast.48, bf16[256,256]{1,0:T(8,128)(2,1)S(1)} %copy-done.6, bf16[256,256]{1,0:T(8,128)(2,1)S(1)} %copy-done.5, bf16[512,512]{1,0:T(8,128)(2,1)S(1)} %copy-done.2, bf16[512,512]{1,0:T(8,128)(2,1)S(1)} %copy-done.1, ...), custom_call_target="tpu_custom_call" | custom-call | tf_op jit(solution)/shard_map/image/pallas_call | solution.py:313
  (24 shorter events, 0.3 us)
Async XLA Ops:
  4.7 24.8 %collective-permute-start = (f32[4,2,128,128]{3,2,1,0:T(8,128)S(1)}, f32[4,2,128,128]{3,2,1,0:T(8,128)S(1)}, u32[]{:S(2)}, u32[]{:S(2)}) collective-permute-start(f32[4,2,128,128]{3,2,1,0:T(8,128)S(1)} %get-tuple-element.9), channel_id=1, source_target_pairs={{0,1},{1,2},{2,3},{3,4},{4,5},{5,6},{6,7},{7,8},{8,9},{9,10},{10,1... | collective-permute-start | bytes 1572872 | tf_op jit(solution)/shard_map/ppermute | solution.py:334
  10.0 8.0 %copy-start = (bf16[6,512,512]{2,1,0:T(8,128)(2,1)S(1)}, bf16[6,512,512]{2,1,0:T(8,128)(2,1)}, u32[]{:S(2)}) copy-start(bf16[6,512,512]{2,1,0:T(8,128)(2,1)} %own_ref.1) | copy-start | bytes 9437188
  10.1 9.0 %collective-permute-start.5 = (f32[2,384,128]{2,1,0:T(8,128)S(1)}, f32[2,384,128]{2,1,0:T(8,128)S(1)}, u32[]{:S(2)}, u32[]{:S(2)}) collective-permute-start(f32[2,384,128]{2,1,0:T(8,128)S(1)} %pad_maximum_fusion.1), channel_id=1, source_target_pairs={{0,192},{64,128},{128,64},{192,0},{1,193},{65,129},{129,65},{193,1... | collective-permute-start | bytes 1179656 | tf_op jit(solution)/shard_map/ppermute | solution.py:326
  12.7 12.5 %collective-permute-start.4 = (f32[2,384,128]{2,1,0:T(8,128)S(1)}, f32[2,384,128]{2,1,0:T(8,128)S(1)}, u32[]{:S(2)}, u32[]{:S(2)}) collective-permute-start(f32[2,384,128]{2,1,0:T(8,128)S(1)} %pad_maximum_fusion), channel_id=1, source_target_pairs={{0,64},{64,0},{128,192},{192,128},{1,65},{65,1},{129,193},{193,129... | collective-permute-start | bytes 1179656 | tf_op jit(solution)/shard_map/ppermute | solution.py:326
  25.2 7.6 %collective-permute-start.6 = (f32[384,128]{1,0:T(8,128)S(1)}, f32[384,128]{1,0:T(8,128)S(1)}, u32[]{:S(2)}, u32[]{:S(2)}) collective-permute-start(f32[384,128]{1,0:T(8,128)S(1)} %get-tuple-element.11), channel_id=1, source_target_pairs={{0,192},{64,128},{128,64},{192,0},{1,193},{65,129},{129,65},{193,1... | collective-permute-start | bytes 589832 | tf_op jit(solution)/shard_map/ppermute | solution.py:326
  28.6 4.8 %collective-permute-start.7 = (f32[384,128]{1,0:T(8,128)S(1)}, f32[384,128]{1,0:T(8,128)S(1)}, u32[]{:S(2)}, u32[]{:S(2)}) collective-permute-start(f32[384,128]{1,0:T(8,128)S(1)} %get-tuple-element.12), channel_id=1, source_target_pairs={{0,64},{64,0},{128,192},{192,128},{1,65},{65,1},{129,193},{193,129... | collective-permute-start | bytes 589832 | tf_op jit(solution)/shard_map/ppermute | solution.py:326
  29.6 6.7 %collective-permute-start.3 = (f32[2,128,128]{2,1,0:T(8,128)S(1)}, f32[2,128,128]{2,1,0:T(8,128)S(1)}, u32[]{:S(2)}, u32[]{:S(2)}) collective-permute-start(f32[2,128,128]{2,1,0:T(8,128)S(1)} %get-tuple-element.17), channel_id=1, source_target_pairs={{0,128},{64,192},{128,0},{192,64},{1,129},{65,193},{129,1},{193,65... | collective-permute-start | bytes 393224 | tf_op jit(solution)/shard_map/ppermute | solution.py:326
  30.2 7.0 %collective-permute-start.2 = (f32[2,128,128]{2,1,0:T(8,128)S(1)}, f32[2,128,128]{2,1,0:T(8,128)S(1)}, u32[]{:S(2)}, u32[]{:S(2)}) collective-permute-start(f32[2,128,128]{2,1,0:T(8,128)S(1)} %get-tuple-element.18), channel_id=1, source_target_pairs={{0,192},{64,128},{128,64},{192,0},{1,193},{65,129},{129,65},{193,1... | collective-permute-start | bytes 393224 | tf_op jit(solution)/shard_map/ppermute | solution.py:326
  32.7 6.1 %collective-permute-start.1 = (f32[2,128,128]{2,1,0:T(8,128)S(1)}, f32[2,128,128]{2,1,0:T(8,128)S(1)}, u32[]{:S(2)}, u32[]{:S(2)}) collective-permute-start(f32[2,128,128]{2,1,0:T(8,128)S(1)} %get-tuple-element.19), channel_id=1, source_target_pairs={{0,64},{64,0},{128,192},{192,128},{1,65},{65,1},{129,193},{193,129... | collective-permute-start | bytes 393224 | tf_op jit(solution)/shard_map/ppermute | solution.py:326
  38.8 33.5 %copy-start.1 = (bf16[512,512]{1,0:T(8,128)(2,1)S(1)}, bf16[512,512]{1,0:T(8,128)(2,1)}, u32[]{:S(2)}) copy-start(bf16[512,512]{1,0:T(8,128)(2,1)} %constant.15.clone.s_lo) | copy-start | bytes 1572868
  38.8 33.5 %copy-start.2 = (bf16[512,512]{1,0:T(8,128)(2,1)S(1)}, bf16[512,512]{1,0:T(8,128)(2,1)}, u32[]{:S(2)}) copy-start(bf16[512,512]{1,0:T(8,128)(2,1)} %constant.14.clone.s_hi) | copy-start | bytes 1572868
  38.8 33.5 %copy-start.3 = (f32[128,256]{1,0:T(8,128)S(1)}, f32[128,256]{1,0:T(8,128)}, u32[]{:S(2)}) copy-start(f32[128,256]{1,0:T(8,128)} %constant.17.clone.tw_s) | copy-start | bytes 393220
  38.8 33.5 %copy-start.4 = (f32[128,256]{1,0:T(8,128)S(1)}, f32[128,256]{1,0:T(8,128)}, u32[]{:S(2)}) copy-start(f32[128,256]{1,0:T(8,128)} %constant.16.clone.tw_c) | copy-start | bytes 393220
  38.8 33.5 %copy-start.5 = (bf16[256,256]{1,0:T(8,128)(2,1)S(1)}, bf16[256,256]{1,0:T(8,128)(2,1)}, u32[]{:S(2)}) copy-start(bf16[256,256]{1,0:T(8,128)(2,1)} %constant.13.clone.f_lo) | copy-start | bytes 393220
  38.8 33.5 %copy-start.6 = (bf16[256,256]{1,0:T(8,128)(2,1)S(1)}, bf16[256,256]{1,0:T(8,128)(2,1)}, u32[]{:S(2)}) copy-start(bf16[256,256]{1,0:T(8,128)(2,1)} %constant.12.clone.f_hi) | copy-start | bytes 393220
  38.8 33.5 %copy-start.7 = (s32[2,2]{1,0:T(2,128)S(1)}, s32[2,2]{1,0:T(2,128)}, u32[]{:S(2)}) copy-start(s32[2,2]{1,0:T(2,128)} %edges.1) | copy-start | bytes 52
